TPU v7x, 128 devices: a whole 4x4x4 slice. The times are simulated.
128 devices in a mesh: dp: 64 (over z, y, x), tp: 2 (over core).
Axes of the slice: x: 4, y: 4, z: 4, core: 2. Of those that a mesh axis runs over, the one named last changes fastest.
Arguments:
- x_teach: bfloat16 [128, 128, 1024], P('dp', 'tp')
- x_stud: bfloat16 [128, 128, 384], P(('dp', 'tp'))
- w_up_t: bfloat16 [32, 1024, 4096], P(None, None, 'tp')
- w_down_t: bfloat16 [32, 4096, 1024], P(None, 'tp')
- gain_t: float32 [32, 1024], replicated
- head_t: bfloat16 [1024, 30592], P(None, 'tp')
- w_up_s: bfloat16 [2, 384, 1536], replicated
- w_down_s: bfloat16 [2, 1536, 384], replicated
- gain_s: float32 [2, 384], replicated
- proj_s: bfloat16 [2, 384, 1024], replicated
- head_s: bfloat16 [384, 30592], replicated
Outputs:
- output 1: float32 [], replicated
- output 2: float32 [2, 384, 1536], replicated
- output 3: float32 [2, 1536, 384], replicated
- output 4: float32 [2, 384], replicated
- output 5: float32 [2, 384, 1024], replicated
- output 6: float32 [384, 30592], replicated
All inputs are finite; a program needn't handle non-finite values.
Results may differ from a plain program's by a relative error of at most 0.00469935.
Values are sent between devices in bfloat16 or wider.
A program may use at most 1.5 GiB of HBM per device.

v0:
```python
import jax
import jax.numpy as jnp
from jax import lax
from jax.sharding import PartitionSpec as P

NORM_EPS = 1e-6


def rms_parts(values):
    vals32 = values.astype(jnp.float32)
    inv_rms = lax.rsqrt(jnp.mean(vals32 * vals32, axis=-1, keepdims=True) + NORM_EPS)
    return vals32 * inv_rms, inv_rms


def rms_back(normed, inv_rms, grad_out):
    return inv_rms * (grad_out - normed * jnp.mean(grad_out * normed, axis=-1, keepdims=True))


def gelu_tanh(values):
    return jax.nn.gelu(values, approximate=True)


def gelu_back(pre_act, grad_out):
    return jax.vjp(gelu_tanh, pre_act)[1](grad_out)[0]


def mat_mul(subscripts, lhs_arr, rhs_arr):
    return jnp.einsum(subscripts, lhs_arr, rhs_arr, preferred_element_type=jnp.float32)


def student_forward(x_stud, w_up_s, w_down_s, gain_s, proj_s, features):
    residual = x_stud.astype(jnp.float32)
    norm_cur, inv_cur = rms_parts(residual)
    saved_acts = []
    err_total = jnp.zeros((), jnp.float32)
    for layer_idx in range(w_up_s.shape[0]):
        normed = (norm_cur * gain_s[layer_idx]).astype(jnp.bfloat16)
        pre_act = mat_mul('bsd,df->bsf', normed, w_up_s[layer_idx])
        hidden_act = gelu_tanh(pre_act).astype(jnp.bfloat16)
        residual = residual + mat_mul('bsf,fd->bsd', hidden_act, w_down_s[layer_idx])
        norm_next, inv_next = rms_parts(residual)
        proj_in = norm_next.astype(jnp.bfloat16)
        feat_err = mat_mul('bsd,de->bse', proj_in, proj_s[layer_idx]) - features[layer_idx]
        err_total = err_total + jnp.sum(feat_err * feat_err)
        saved_acts.append((norm_cur, inv_cur, normed, pre_act, hidden_act, norm_next, inv_next, proj_in, feat_err))
        norm_cur, inv_cur = norm_next, inv_next
    return saved_acts, err_total


def student_backward(saved_acts, w_up_s, w_down_s, gain_s, proj_s, feat_coef, head_in_grad):
    n_layers = len(saved_acts)
    up_grads = []
    down_grads = []
    gain_grads = []
    proj_grads = []
    resid_grad = None
    for layer_idx in reversed(range(n_layers)):
        norm_cur, inv_cur, normed, pre_act, hidden_act, norm_next, inv_next, proj_in, feat_err = saved_acts[layer_idx]
        err_grad = (2.0 * feat_coef * feat_err).astype(jnp.bfloat16)
        proj_grads.append(mat_mul('bsd,bse->de', proj_in, err_grad))
        out_grad = mat_mul('bse,de->bsd', err_grad, proj_s[layer_idx])
        if resid_grad is None:
            resid_grad = rms_back(norm_next, inv_next, out_grad + head_in_grad)
        else:
            resid_grad = resid_grad + rms_back(norm_next, inv_next, out_grad)
        resid_bf = resid_grad.astype(jnp.bfloat16)
        down_grads.append(mat_mul('bsf,bsd->fd', hidden_act, resid_bf))
        act_grad = mat_mul('bsd,fd->bsf', resid_bf, w_down_s[layer_idx])
        pre_grad = gelu_back(pre_act, act_grad).astype(jnp.bfloat16)
        up_grads.append(mat_mul('bsd,bsf->df', normed, pre_grad))
        norm_grad = mat_mul('bsf,df->bsd', pre_grad, w_up_s[layer_idx])
        gain_grads.append(jnp.sum(norm_grad * norm_cur, axis=(0, 1)))
        if layer_idx > 0:
            resid_grad = resid_grad + rms_back(norm_cur, inv_cur, norm_grad * gain_s[layer_idx])
    return (jnp.stack(up_grads[::-1]), jnp.stack(down_grads[::-1]),
            jnp.stack(gain_grads[::-1]), jnp.stack(proj_grads[::-1]))


def solution(mesh):
    dp_size = mesh.shape['dp']
    tp_size = mesh.shape['tp']

    def local_step(x_teach, x_stud, w_up_t, w_down_t, gain_t, head_t, w_up_s, w_down_s, gain_s, proj_s, head_s):
        n_feat = w_up_s.shape[0]
        per_feat = w_up_t.shape[0] // n_feat
        hidden = x_teach
        features = []
        for layer_idx in range(w_up_t.shape[0]):
            normed = (rms_parts(hidden)[0] * gain_t[layer_idx]).astype(jnp.bfloat16)
            gathered = lax.all_gather(normed, 'tp', axis=1, tiled=True)
            hidden_act = gelu_tanh(mat_mul('bsd,df->bsf', gathered, w_up_t[layer_idx])).astype(jnp.bfloat16)
            partial_out = mat_mul('bsf,fd->bsd', hidden_act, w_down_t[layer_idx])
            layer_out = lax.psum_scatter(partial_out, 'tp', scatter_dimension=1, tiled=True)
            hidden = hidden + layer_out.astype(jnp.bfloat16)
            if (layer_idx + 1) % per_feat == 0:
                features.append(lax.all_to_all(hidden, 'tp', 0, 1, tiled=True))
        final_norm = rms_parts(hidden)[0].astype(jnp.bfloat16)
        final_full = lax.all_gather(final_norm, 'tp', axis=1, tiled=True)
        teach_logits = mat_mul('bsd,dv->bsv', final_full, head_t)

        n_tokens = x_stud.shape[0] * x_stud.shape[1] * dp_size * tp_size
        feat_coef = 1.0 / (n_feat * n_tokens * head_t.shape[0])
        kl_coef = 1.0 / n_tokens
        saved_acts, err_total = student_forward(x_stud, w_up_s, w_down_s, gain_s, proj_s, features)
        head_in = saved_acts[-1][7]
        stud_full = lax.all_gather(head_in, 'tp', axis=0, tiled=True)
        vocab_part = head_t.shape[1]
        head_cols = lax.dynamic_slice_in_dim(head_s, lax.axis_index('tp') * vocab_part, vocab_part, axis=1)
        stud_logits = mat_mul('bsd,dv->bsv', stud_full, head_cols)
        peak_vals = lax.pmax(jnp.stack([jnp.max(teach_logits, axis=-1), jnp.max(stud_logits, axis=-1)]), 'tp')
        teach_exp = jnp.exp(teach_logits - peak_vals[0][..., None])
        stud_exp = jnp.exp(stud_logits - peak_vals[1][..., None])
        sum_vals = lax.psum(jnp.stack([jnp.sum(teach_exp, axis=-1), jnp.sum(stud_exp, axis=-1)]), 'tp')
        log_norms = peak_vals + jnp.log(sum_vals)
        teach_prob = teach_exp / sum_vals[0][..., None]
        stud_prob = stud_exp / sum_vals[1][..., None]
        log_ratio = teach_logits - stud_logits - (log_norms[0] - log_norms[1])[..., None]
        kl_local = jnp.sum(teach_prob * log_ratio)
        logit_grad = (kl_coef * (stud_prob - teach_prob)).astype(jnp.bfloat16)
        head_part = mat_mul('bsd,bsv->dv', stud_full, logit_grad)
        head_grad = lax.all_gather(lax.psum(head_part, 'dp'), 'tp', axis=1, tiled=True)
        full_in_grad = mat_mul('bsv,dv->bsd', logit_grad, head_cols)
        head_in_grad = lax.psum_scatter(full_in_grad, 'tp', scatter_dimension=0, tiled=True)
        local_grads = student_backward(saved_acts, w_up_s, w_down_s, gain_s, proj_s, feat_coef, head_in_grad)
        grad_up, grad_down, grad_gain, grad_proj = lax.psum(local_grads, ('dp', 'tp'))
        total_loss = lax.psum(feat_coef * err_total + kl_coef * kl_local, ('dp', 'tp'))
        return total_loss, grad_up, grad_down, grad_gain, grad_proj, head_grad

    in_specs = (P('dp', 'tp', None), P(('dp', 'tp'), None, None), P(None, None, 'tp'), P(None, 'tp', None),
                P(), P(None, 'tp'), P(), P(), P(), P(), P())
    out_specs = (P(), P(), P(), P(), P(), P())
    return jax.shard_map(local_step, mesh=mesh, in_specs=in_specs, out_specs=out_specs, check_vma=False)
```

profile of v0, /device:TPU:1, one launch (start us, length us, event | category | flops | bytes accessed | tf_op | source)
XLA Modules:
  0.0 1367.5 jit_solution(16309487388918927568)
XLA Ops:
  21.4 13.8 %reduce-scatter.34.cloned.1.call-done = f32[2,64,1024]{2,1,0:T(8,128)} async-done(((f32[2,128,1024]{2,1,0:T(8,128)}), f32[2,64,1024]{2,1,0:T(8,128)}) %reduce-scatter.34.cloned.1.call-update) | async-done | bytes 524304 | tf_op jit(solution)/shard_map/reduce_scatter | solution.py:93
  69.0 12.5 reduce-scatter.38.cloned.1.call-done
  92.1 12.5 reduce-scatter.40.cloned.1.call-done
  115.6 12.5 reduce-scatter.42.cloned.1.call-done
  138.7 12.5 reduce-scatter.44.cloned.1.call-done
  161.8 12.5 reduce-scatter.46.cloned.1.call-done
  184.9 12.5 reduce-scatter.48.cloned.1.call-done
  208.2 12.5 reduce-scatter.50.cloned.1.call-done
  231.3 12.5 reduce-scatter.52.cloned.1.call-done
  254.4 12.5 reduce-scatter.54.cloned.1.call-done
  300.9 12.5 reduce-scatter.58.cloned.1.call-done
  324.0 12.5 reduce-scatter.60.cloned.1.call-done
  347.1 12.5 reduce-scatter.62.cloned.1.call-done
  370.2 12.5 reduce-scatter.64.cloned.1.call-done
  393.7 12.5 reduce-scatter.66.cloned.1.call-done
  416.8 12.5 reduce-scatter.68.cloned.1.call-done
  439.9 12.5 reduce-scatter.70.cloned.1.call-done
  463.0 12.5 reduce-scatter.72.cloned.1.call-done
  509.4 12.5 reduce-scatter.76.cloned.1.call-done
  532.5 12.5 reduce-scatter.78.cloned.1.call-done
  555.6 12.5 reduce-scatter.80.cloned.1.call-done
  578.9 12.5 reduce-scatter.82.cloned.1.call-done
  625.1 12.5 reduce-scatter.86.cloned.1.call-done
  694.8 12.5 reduce-scatter.92.cloned.1.call-done
  747.7 17.4 %fusion.984 = (f32[2,128]{1,0:T(2,128)S(1)}, f32[2,128,15296]{1,2,0:T(8,128)}) fusion(bf16[2,128,384]{2,1,0:T(8,128)(2,1)S(1)} %all_gather.138, bf16[384,30592]{1,0:T(8,128)(2,1)} %param.21, s32[]{:T(128)S(6)} %select_n.3), kind=kOutput, calls=%fused_computation.989 | convolution fusion | flops 3011231488 | bytes 27657220 | tf_op jit(solution)/shard_map/bsd,dv->bsv/dot_general | solution.py:28
  768.6 19.9 %fusion.985 = (f32[2,128]{1,0:T(2,128)S(1)}, f32[2,128,15296]{1,2,0:T(8,128)}) fusion(bf16[2,128,1024]{2,1,0:T(8,128)(2,1)S(1)} %all_gather.137, bf16[1024,15296]{0,1:T(8,128)(2,1)} %param.16), kind=kOutput, calls=%fused_computation.990 | convolution fusion | flops 8023425024 | bytes 47514624 | tf_op jit(solution)/shard_map/bsd,dv->bsv/dot_general | solution.py:28
  805.0 13.5 multiply_convert_fusion
  832.1 15.7 %fusion.5 = f32[2,128,384]{2,1,0:T(8,128)} fusion(bf16[2,128,15296]{1,2,0:T(8,128)(2,1)} %copy-done, bf16[384,30592]{1,0:T(8,128)(2,1)} %param.21, s32[]{:T(128)S(6)} %select_n.3), kind=kOutput, calls=%fused_computation.10 | convolution fusion | flops 3007315968 | bytes 20021252 | tf_op jit(solution)/shard_map/bsv,dv->bsd/dot_general | solution.py:28
  847.9 238.3 %all-reduce.5.cloned.1.call-done = f32[384,15296]{0,1:T(8,128)} async-done(((f32[384,15296]{0,1:T(8,128)}), f32[384,15296]{0,1:T(8,128)}) %all-reduce.5.cloned.1.call-update) | async-done | bytes 23494672 | tf_op jit(solution)/shard_map/psum | solution.py:121
  1119.2 64.7 %all-reduce = (f32[]{:T(128)}, f32[2,384]{1,0:T(2,128)}) all-reduce(f32[]{:T(128)S(6)} %add.846, f32[2,384]{1,0:T(2,128)S(1)} %pad_maximum_fusion.3), channel_id=1, replica_groups=mesh['dp'=64,'tp'=2] {'dp','tp'}, use_global_device_ids=true, to_apply=%region_77.0 | all-reduce | flops 769 | bytes 6152 | tf_op jit(solution)/shard_map/psum | solution.py:126
  1183.9 45.8 %copy.20 = f32[384,30592]{1,0:T(8,128)} copy(f32[384,30592]{0,1:T(8,128)} %all-gather.2.cloned.1.call-done) | data formatting | bytes 93978624
  1229.7 120.5 %all-reduce.7.cloned.1.call-done = (f32[2,384,1536]{2,1,0:T(8,128)}, f32[2,1536,384]{2,1,0:T(8,128)}, f32[2,384,1024]{2,1,0:T(8,128)}) async-done(((f32[2,384,1536]{2,1,0:T(8,128)}, f32[2,1536,384]{2,1,0:T(8,128)}, f32[2,384,1024]{2,1,0:T(8,128)}), (f32[2,384,1536]{2,1,0:T(8,128)}, f32[2,1536,384]{2,1,0:T(8,128)}, f32[2,384,1024]{2,1,0:T(8,128)})) %all-reduce.7.cloned.1.call-update) | async-done | bytes 12582928 | tf_op jit(solution)/shard_map/psum | solution.py:125
  (347 shorter events, 513.5 us)
Async XLA Ops:
  21.4 37.0 %reduce-scatter.36.cloned.1.call-start = ((), (), s32[]{:S(2)}) async-start(), calls=%async_computation.36 | async-start | bytes 1572864 | tf_op jit(solution)/shard_map/reduce_scatter | solution.py:93
  68.9 35.6 %reduce-scatter.40.cloned.1.call-start = ((), (), s32[]{:S(2)}) async-start(), calls=%async_computation.38 | async-start | bytes 1572864 | tf_op jit(solution)/shard_map/reduce_scatter | solution.py:93
  92.0 36.1 %reduce-scatter.42.cloned.1.call-start = ((), (), s32[]{:S(2)}) async-start(), calls=%async_computation.39 | async-start | bytes 1572864 | tf_op jit(solution)/shard_map/reduce_scatter | solution.py:93
  115.6 35.6 %reduce-scatter.44.cloned.1.call-start = ((), (), s32[]{:S(2)}) async-start(), calls=%async_computation.40 | async-start | bytes 1572864 | tf_op jit(solution)/shard_map/reduce_scatter | solution.py:93
  138.7 35.6 %reduce-scatter.46.cloned.1.call-start = ((), (), s32[]{:S(2)}) async-start(), calls=%async_computation.41 | async-start | bytes 1572864 | tf_op jit(solution)/shard_map/reduce_scatter | solution.py:93
  161.8 35.6 %reduce-scatter.48.cloned.1.call-start = ((), (), s32[]{:S(2)}) async-start(), calls=%async_computation.42 | async-start | bytes 1572864 | tf_op jit(solution)/shard_map/reduce_scatter | solution.py:93
  184.9 35.8 %reduce-scatter.50.cloned.1.call-start = ((), (), s32[]{:S(2)}) async-start(), calls=%async_computation.43 | async-start | bytes 1572864 | tf_op jit(solution)/shard_map/reduce_scatter | solution.py:93
  208.1 35.6 %reduce-scatter.52.cloned.1.call-start = ((), (), s32[]{:S(2)}) async-start(), calls=%async_computation.44 | async-start | bytes 1572864 | tf_op jit(solution)/shard_map/reduce_scatter | solution.py:93
  254.3 35.7 %reduce-scatter.56.cloned.1.call-start = ((), (), s32[]{:S(2)}) async-start(), calls=%async_computation.46 | async-start | bytes 1572864 | tf_op jit(solution)/shard_map/reduce_scatter | solution.py:93
  277.5 35.8 %reduce-scatter.58.cloned.1.call-start = ((), (), s32[]{:S(2)}) async-start(), calls=%async_computation.47 | async-start | bytes 1572864 | tf_op jit(solution)/shard_map/reduce_scatter | solution.py:93
  300.8 35.6 %reduce-scatter.60.cloned.1.call-start = ((), (), s32[]{:S(2)}) async-start(), calls=%async_computation.48 | async-start | bytes 1572864 | tf_op jit(solution)/shard_map/reduce_scatter | solution.py:93
  323.9 35.6 %reduce-scatter.62.cloned.1.call-start = ((), (), s32[]{:S(2)}) async-start(), calls=%async_computation.49 | async-start | bytes 1572864 | tf_op jit(solution)/shard_map/reduce_scatter | solution.py:93
  347.0 35.7 %reduce-scatter.64.cloned.1.call-start = ((), (), s32[]{:S(2)}) async-start(), calls=%async_computation.50 | async-start | bytes 1572864 | tf_op jit(solution)/shard_map/reduce_scatter | solution.py:93
  370.1 36.0 %reduce-scatter.66.cloned.1.call-start = ((), (), s32[]{:S(2)}) async-start(), calls=%async_computation.51 | async-start | bytes 1572864 | tf_op jit(solution)/shard_map/reduce_scatter | solution.py:93
  393.7 35.6 %reduce-scatter.68.cloned.1.call-start = ((), (), s32[]{:S(2)}) async-start(), calls=%async_computation.52 | async-start | bytes 1572864 | tf_op jit(solution)/shard_map/reduce_scatter | solution.py:93
  416.8 35.6 %reduce-scatter.70.cloned.1.call-start = ((), (), s32[]{:S(2)}) async-start(), calls=%async_computation.53 | async-start | bytes 1572864 | tf_op jit(solution)/shard_map/reduce_scatter | solution.py:93
  439.9 35.6 %reduce-scatter.72.cloned.1.call-start = ((), (), s32[]{:S(2)}) async-start(), calls=%async_computation.54 | async-start | bytes 1572864 | tf_op jit(solution)/shard_map/reduce_scatter | solution.py:93
  463.0 35.8 %reduce-scatter.74.cloned.1.call-start = ((), (), s32[]{:S(2)}) async-start(), calls=%async_computation.55 | async-start | bytes 1572864 | tf_op jit(solution)/shard_map/reduce_scatter | solution.py:93
  486.2 35.6 %reduce-scatter.76.cloned.1.call-start = ((), (), s32[]{:S(2)}) async-start(), calls=%async_computation.56 | async-start | bytes 1572864 | tf_op jit(solution)/shard_map/reduce_scatter | solution.py:93
  509.3 35.6 %reduce-scatter.78.cloned.1.call-start = ((), (), s32[]{:S(2)}) async-start(), calls=%async_computation.57 | async-start | bytes 1572864 | tf_op jit(solution)/shard_map/reduce_scatter | solution.py:93
  532.4 35.6 %reduce-scatter.80.cloned.1.call-start = ((), (), s32[]{:S(2)}) async-start(), calls=%async_computation.58 | async-start | bytes 1572864 | tf_op jit(solution)/shard_map/reduce_scatter | solution.py:93
  555.5 35.8 %reduce-scatter.82.cloned.1.call-start = ((), (), s32[]{:S(2)}) async-start(), calls=%async_computation.59 | async-start | bytes 1572864 | tf_op jit(solution)/shard_map/reduce_scatter | solution.py:93
  578.8 35.6 %reduce-scatter.84.cloned.1.call-start = ((), (), s32[]{:S(2)}) async-start(), calls=%async_computation.60 | async-start | bytes 1572864 | tf_op jit(solution)/shard_map/reduce_scatter | solution.py:93
  601.9 35.7 %reduce-scatter.86.cloned.1.call-start = ((), (), s32[]{:S(2)}) async-start(), calls=%async_computation.61 | async-start | bytes 1572864 | tf_op jit(solution)/shard_map/reduce_scatter | solution.py:93
  648.2 36.0 %reduce-scatter.90.cloned.1.call-start = ((), (), s32[]{:S(2)}) async-start(), calls=%async_computation.63 | async-start | bytes 1572864 | tf_op jit(solution)/shard_map/reduce_scatter | solution.py:93
  671.7 35.6 %reduce-scatter.92.cloned.1.call-start = ((), (), s32[]{:S(2)}) async-start(), calls=%async_computation.64 | async-start | bytes 1572864 | tf_op jit(solution)/shard_map/reduce_scatter | solution.py:93
  694.8 35.7 %reduce-scatter.94.cloned.1.call-start = ((), (), s32[]{:S(2)}) async-start(), calls=%async_computation.65 | async-start | bytes 1572864 | tf_op jit(solution)/shard_map/reduce_scatter | solution.py:93
  717.9 47.1 %reduce-scatter.96.cloned.1.call-start = ((), (), s32[]{:S(2)}) async-start(), calls=%async_computation.66 | async-start | bytes 1572864 | tf_op jit(solution)/shard_map/reduce_scatter | solution.py:93
  741.0 345.1 %all-reduce.5.cloned.1.call-start = ((), (), s32[]{:S(2)}) async-start(), calls=%async_computation.68 | async-start | bytes 46989312 | tf_op jit(solution)/shard_map/psum | solution.py:121
  832.1 270.7 %reduce-scatter.98.cloned.1.call-start = ((), (), s32[]{:S(2)}) async-start(), calls=%async_computation.67 | async-start | bytes 589824 | tf_op jit(solution)/shard_map/reduce_scatter | solution.py:123
  847.9 336.0 %all-gather.2.cloned.1.call-start = ((), (), s32[]{:S(2)}) async-start(), calls=%async_computation.69 | async-start | bytes 70483968 | tf_op jit(solution)/shard_map/all_gather | solution.py:121
  1086.2 264.0 %all-reduce.7.cloned.1.call-start = ((), (), s32[]{:S(2)}) async-start(), calls=%async_computation.70 | async-start | bytes 25165824 | tf_op jit(solution)/shard_map/psum | solution.py:125
  (28 other events, 277.2 us)
Sparse Core Ops, SparseCore 0:
  21.5 13.7 reduce-scatter.33
  69.0 12.3 reduce-scatter.37
  92.1 12.3 reduce-scatter.39
  115.7 12.3 reduce-scatter.41
  138.8 12.3 reduce-scatter.43
  161.9 12.3 reduce-scatter.45
  185.0 12.3 reduce-scatter.47
  208.3 12.3 reduce-scatter.49
  231.4 12.3 reduce-scatter.51
  254.5 12.3 reduce-scatter.53
  277.6 12.3 reduce-scatter.55
  300.9 12.3 reduce-scatter.57
  324.0 12.3 reduce-scatter.59
  347.1 12.3 reduce-scatter.61
  370.3 12.3 reduce-scatter.63
  393.8 12.3 reduce-scatter.65
  416.9 12.3 reduce-scatter.67
  440.0 12.3 reduce-scatter.69
  463.1 12.3 reduce-scatter.71
  486.4 12.3 reduce-scatter.73
  509.5 12.3 reduce-scatter.75
  532.6 12.3 reduce-scatter.77
  555.7 12.3 reduce-scatter.79
  579.0 12.3 reduce-scatter.81
  602.1 12.3 reduce-scatter.83
  625.2 12.3 reduce-scatter.85
  648.3 12.3 reduce-scatter.87
  671.8 12.3 reduce-scatter.89
  694.9 12.3 reduce-scatter.91
  832.2 253.9 all-reduce.4
  1102.7 72.6 all-gather.1
  1181.1 169.0 all-reduce.6
  (4 shorter events, 48.7 us)
where the time goes:
time: 1380 us; the launch traced here: 1370 us
  waiting for transfers between devices  744 us (54%)
  matrix products  307 us (22%)
  blocking collectives  157 us (11%)
  other arithmetic  77.3 us (6%)
  local copies, waits for them, and re-layouts  63.8 us (5%)
  between operations  17.5 us (1%)
    reduce_scatter x32, waiting for transfers between devices, local_step(): lax.psum_scatter(partial_out, 'tp', scatter_dimension=1, tiled=True)  384 us
    dot_general x54, matrix products, mat_mul(): jnp.einsum(subscripts, lhs_arr, rhs_arr, preferred_element_type=jnp.float32)  307 us
    psum x1, waiting for transfers between devices, local_step(): lax.psum(head_part, 'dp')  238 us
    psum x1, waiting for transfers between devices, local_step(): lax.psum(local_grads, ('dp', 'tp'))  121 us
    all_gather x32, blocking collectives, local_step(): gathered = lax.all_gather(normed, 'tp', axis=1, tiled=True)  73 us
    psum x1, blocking collectives, local_step(): lax.psum(feat_coef * err_total + kl_coef * kl_local, ('dp', 'tp'))  64.7 us
    unnamed x52, local copies, waits for them, and re-layouts  62 us
    reduce_sum x34, other arithmetic, rms_parts(): jnp.mean(vals32 * vals32, axis=-1, keepdims=True) + NORM_EPS  39.4 us
  transfers between devices with their start and end apart: 36, of which 33 were waited for; matrix products, arithmetic and copies ran while one was open for 8% of the time, Pallas kernels for 0%

commit v1 on v0

--- a/solution.py
+++ b/solution.py
@@ -1,9 +1,14 @@
+import functools
+
 import jax
 import jax.numpy as jnp
 from jax import lax
+from jax.experimental import pallas as pl
+from jax.experimental.pallas import tpu as pltpu
 from jax.sharding import PartitionSpec as P
 
 NORM_EPS = 1e-6
+MESH = pl.DeviceIdType.MESH
 
 
 def rms_parts(values):
@@ -26,6 +31,140 @@
 
 def mat_mul(subscripts, lhs_arr, rhs_arr):
     return jnp.einsum(subscripts, lhs_arr, rhs_arr, preferred_element_type=jnp.float32)
+
+
+def gelu_act(u):
+    inner = u * (0.7978845608028654 + 0.035677408136300125 * (u * u))
+    half = 0.5 * u
+    return half + half * jnp.tanh(inner)
+
+
+def teacher_kernel(n_layers, feat_at, up_blk, dn_blk, slots_w,
+                   x_ref, gain_ref, wup_hbm, wdn_hbm,
+                   feat_ref, hout_ref,
+                   h, nrm, act, wu, wd, part, got,
+                   wsem, xsem, ssem, rsem):
+    me = lax.axis_index('tp')
+    peer = {'tp': 1 - me}
+    rows, seq_half, d_model = x_ref.shape
+    n_tok = 2 * seq_half
+    d_ff = wu.shape[-1]
+    n_up = d_ff // up_blk
+    n_dn = d_model // dn_blk
+
+    def up_copy(layer, slot):
+        return pltpu.make_async_copy(wup_hbm.at[layer], wu.at[slot], wsem.at[0, slot])
+
+    def down_copy(layer, slot):
+        return pltpu.make_async_copy(wdn_hbm.at[layer], wd.at[slot], wsem.at[1, slot])
+
+    for i in range(slots_w):
+        up_copy(i, i).start()
+        down_copy(i, i).start()
+
+    barrier = pltpu.get_barrier_semaphore()
+    pl.semaphore_signal(barrier, inc=1, device_id=peer, device_id_type=MESH)
+    pl.semaphore_wait(barrier, 1)
+
+    mine = pl.ds(pl.multiple_of(me * seq_half, seq_half), seq_half)
+    xcopy = pltpu.make_async_remote_copy(
+        src_ref=x_ref, dst_ref=h.at[:, mine], send_sem=xsem.at[0], recv_sem=xsem.at[1],
+        device_id=peer, device_id_type=MESH)
+    xcopy.start()
+    h[:, mine] = x_ref[...]
+    xcopy.wait()
+
+    def p_copy(ck, slot, n):
+        return pltpu.make_async_remote_copy(
+            src_ref=part.at[ck, slot, n], dst_ref=got.at[ck, slot, n],
+            send_sem=ssem.at[ck, slot, n], recv_sem=rsem.at[ck, slot, n],
+            device_id=peer, device_id_type=MESH)
+
+    def update(ck, slot):
+        for n in range(n_dn):
+            p_copy(ck, slot, n).wait()
+            cols = slice(n * dn_blk, (n + 1) * dn_blk)
+            total = part[ck, slot, n] + got[ck, slot, n]
+            new = h[ck, :, cols].astype(jnp.float32) + total.astype(jnp.bfloat16).astype(jnp.float32)
+            h[ck, :, cols] = new.astype(jnp.bfloat16)
+
+    def layer_step(layer, _):
+        slot = lax.rem(layer, 2)
+        prev = 1 - slot
+        ws = lax.rem(layer, slots_w)
+        for ck in range(rows):
+            @pl.when(layer > 0)
+            def _():
+                update(ck, prev)
+
+            @pl.when((layer == feat_at) & (me == ck))
+            def _():
+                feat_ref[...] = h[ck]
+
+            hv = h[ck].astype(jnp.float32)
+            inv = lax.rsqrt(jnp.mean(hv * hv, axis=-1, keepdims=True) + NORM_EPS)
+            nrm[...] = ((hv * inv) * gain_ref[pl.ds(layer, 1), :]).astype(jnp.bfloat16)
+            if ck == 0:
+                up_copy(layer, ws).wait()
+            for n in range(n_up):
+                cols = slice(n * up_blk, (n + 1) * up_blk)
+                u = jnp.dot(nrm[...], wu[ws, :, cols], preferred_element_type=jnp.float32)
+                act[:, cols] = gelu_act(u).astype(jnp.bfloat16)
+            if ck == rows - 1:
+                @pl.when(layer + slots_w < n_layers)
+                def _():
+                    up_copy(layer + slots_w, ws).start()
+            if ck == 0:
+                down_copy(layer, ws).wait()
+            for n in range(n_dn):
+                cols = slice(n * dn_blk, (n + 1) * dn_blk)
+                part[ck, slot, n] = jnp.dot(act[...], wd[ws, :, cols], preferred_element_type=jnp.float32)
+                p_copy(ck, slot, n).start()
+            if ck == rows - 1:
+                @pl.when(layer + slots_w < n_layers)
+                def _():
+                    down_copy(layer + slots_w, ws).start()
+        return 0
+
+    lax.fori_loop(0, n_layers, layer_step, 0)
+    last = (n_layers - 1) % 2
+    for ck in range(rows):
+        update(ck, last)
+        hout_ref[ck] = h[ck]
+
+
+def teacher(x_teach, gain_t, w_up_t, w_down_t, feat_at, up_blk=2048, dn_blk=1024, slots_w=3, collective_id=0):
+    n_layers, d_model, d_ff = w_up_t.shape
+    rows, seq_half, _ = x_teach.shape
+    n_tok = 2 * seq_half
+    n_dn = d_model // dn_blk
+    f32, bf = jnp.float32, jnp.bfloat16
+    vm = pl.BlockSpec(memory_space=pltpu.VMEM)
+    hb = pl.BlockSpec(memory_space=pl.ANY)
+    flops = 2 * 2 * rows * n_tok * d_model * d_ff * n_layers
+    return pl.pallas_call(
+        functools.partial(teacher_kernel, n_layers, feat_at, up_blk, dn_blk, slots_w),
+        out_shape=(jax.ShapeDtypeStruct((n_tok, d_model), bf), jax.ShapeDtypeStruct((rows, n_tok, d_model), bf)),
+        in_specs=[vm, vm, hb, hb],
+        out_specs=(vm, vm),
+        scratch_shapes=[
+            pltpu.VMEM((rows, n_tok, d_model), bf),
+            pltpu.VMEM((n_tok, d_model), bf),
+            pltpu.VMEM((n_tok, d_ff), bf),
+            pltpu.VMEM((slots_w, d_model, d_ff), bf),
+            pltpu.VMEM((slots_w, d_ff, d_model), bf),
+            pltpu.VMEM((rows, 2, n_dn, n_tok, dn_blk), f32),
+            pltpu.VMEM((rows, 2, n_dn, n_tok, dn_blk), f32),
+            pltpu.SemaphoreType.DMA((2, slots_w)),
+            pltpu.SemaphoreType.DMA((2,)),
+            pltpu.SemaphoreType.DMA((rows, 2, n_dn)),
+            pltpu.SemaphoreType.DMA((rows, 2, n_dn)),
+        ],
+        compiler_params=pltpu.CompilerParams(collective_id=collective_id, has_side_effects=True,
+                                             vmem_limit_bytes=48 * 1024 * 1024),
+        cost_estimate=pl.CostEstimate(flops=flops, bytes_accessed=4 * n_layers * d_model * d_ff, transcendentals=0),
+        name='teacher',
+    )(x_teach, gain_t, w_up_t, w_down_t)
 
 
 def student_forward(x_stud, w_up_s, w_down_s, gain_s, proj_s, features):
@@ -83,19 +222,10 @@
     def local_step(x_teach, x_stud, w_up_t, w_down_t, gain_t, head_t, w_up_s, w_down_s, gain_s, proj_s, head_s):
         n_feat = w_up_s.shape[0]
         per_feat = w_up_t.shape[0] // n_feat
-        hidden = x_teach
-        features = []
-        for layer_idx in range(w_up_t.shape[0]):
-            normed = (rms_parts(hidden)[0] * gain_t[layer_idx]).astype(jnp.bfloat16)
-            gathered = lax.all_gather(normed, 'tp', axis=1, tiled=True)
-            hidden_act = gelu_tanh(mat_mul('bsd,df->bsf', gathered, w_up_t[layer_idx])).astype(jnp.bfloat16)
-            partial_out = mat_mul('bsf,fd->bsd', hidden_act, w_down_t[layer_idx])
-            layer_out = lax.psum_scatter(partial_out, 'tp', scatter_dimension=1, tiled=True)
-            hidden = hidden + layer_out.astype(jnp.bfloat16)
-            if (layer_idx + 1) % per_feat == 0:
-                features.append(lax.all_to_all(hidden, 'tp', 0, 1, tiled=True))
-        final_norm = rms_parts(hidden)[0].astype(jnp.bfloat16)
-        final_full = lax.all_gather(final_norm, 'tp', axis=1, tiled=True)
+        feat_first, hidden = teacher(x_teach, gain_t, w_up_t, w_down_t, per_feat)
+        own_row = lax.dynamic_slice_in_dim(hidden, lax.axis_index('tp'), 1, axis=0)
+        features = [feat_first[None], own_row]
+        final_full = rms_parts(hidden)[0].astype(jnp.bfloat16)
         teach_logits = mat_mul('bsd,dv->bsv', final_full, head_t)
 
         n_tokens = x_stud.shape[0] * x_stud.shape[1] * dp_size * tp_size

time: 1380 us -> 746 us (0.54)
  waiting for transfers between devices: 744 us -> 353 us
  matrix products: 307 us -> 79.5 us
  Pallas kernels: 0 us -> 116 us
  blocking collectives: 157 us -> 73.6 us
  other arithmetic: 77.3 us -> 33.7 us
    reduce_scatter x32 -> x0, waiting for transfers between devices: 384 us -> none  [local_step(): lax.psum_scatter(partial_out, 'tp', scatter_dimension=1, tiled=True)]
    dot_general x54 -> x22, matrix products: 307 us -> 79.5 us  [mat_mul(): jnp.einsum(subscripts, lhs_arr, rhs_arr, preferred_element_type=jnp.float32)]
    pallas_call x0 -> x1, Pallas kernels: none -> 116 us  [teacher(): pl.pallas_call(functools.partial(teacher_kernel, n_layers, feat_at, up_bl...]
    all_gather x33 -> x0, blocking collectives: 75.1 us -> none  [the longest x32 73 us: local_step(): gathered = lax.all_gather(normed, 'tp', axis=1, tiled=True)]
    reduce_sum x34 -> x2, other arithmetic: 39.4 us -> 1.67 us  [rms_parts(): jnp.mean(vals32 * vals32, axis=-1, keepdims=True) + NORM_EPS]
    unnamed x52 -> x60, local copies, waits for them, and re-layouts: 62 us -> 62.4 us
  transfers between devices with their start and end apart: 36 -> 4, of which waited for: 33 -> 2; matrix products, arithmetic and copies ran while one was open for 8% -> 11% of each run, Pallas kernels for 0% -> 0%
where the time goes in v1:
time: 746 us; the launch traced here: 739 us
  waiting for transfers between devices  353 us (47%)
  Pallas kernels  116 us (16%)
  matrix products  79.5 us (11%)
  blocking collectives  73.6 us (10%)
  local copies, waits for them, and re-layouts  63.3 us (8%)
  other arithmetic  33.7 us (5%)
  between operations  18.6 us (2%)
    psum x1, waiting for transfers between devices, local_step(): lax.psum(head_part, 'dp')  239 us
    pallas_call x1, Pallas kernels, teacher(): pl.pallas_call(functools.partial(teacher_kernel, n_layers, feat_at, up_bl...  116 us
    psum x1, waiting for transfers between devices, local_step(): lax.psum(local_grads, ('dp', 'tp'))  114 us
    dot_general x22, matrix products, mat_mul(): jnp.einsum(subscripts, lhs_arr, rhs_arr, preferred_element_type=jnp.float32)  79.5 us
    psum x1, blocking collectives, local_step(): lax.psum(feat_coef * err_total + kl_coef * kl_local, ('dp', 'tp'))  65.7 us
    unnamed x60, local copies, waits for them, and re-layouts  62.4 us
  transfers between devices with their start and end apart: 4, of which 2 were waited for; matrix products, arithmetic and copies ran while one was open for 11% of the time, Pallas kernels for 0%

profile of v1, /device:TPU:1, one launch (start us, length us, event | category | flops | bytes accessed | tf_op | source)
XLA Modules:
  0.0 738.5 jit_solution(3525564951775449576)
XLA Ops:
  8.1 0.9 slice_reduce_fusion
  9.0 1.5 fusion.91
  10.5 1.7 fusion.26
  12.3 2.1 multiply_reduce_fusion.6
  15.3 0.9 copy-done.8
  17.5 2.9 all_gather.6
  20.4 115.8 %teacher.1 = (bf16[128,1024]{1,0:T(8,128)(2,1)S(1)}, bf16[2,128,1024]{2,1,0:T(8,128)(2,1)S(1)}) custom-call(bf16[2,64,1024]{2,1,0:T(8,128)(2,1)S(1)} %copy-done, f32[32,1024]{1,0:T(8,128)S(1)} %copy-done.1, bf16[32,1024,2048]{2,1,0:T(8,128)(2,1)} %wup_hbm.1, bf16[32,2048,1024]{2,1,0:T(8,128)(2,1)} %wdn_hbm.1), custom_call_target="tpu_custom_call" | custom-call | flops 68719476736 | bytes 268435456 | tf_op jit(solution)/shard_map/teacher/pallas_call | solution.py:145
  136.4 20.1 %fusion.125 = (f32[2,128]{1,0:T(2,128)S(1)}, f32[2,128,15296]{1,2,0:T(8,128)}) fusion(bf16[1024,15296]{0,1:T(8,128)(2,1)} %param.16, bf16[2,128,1024]{2,1,0:T(8,128)(2,1)S(1)} %get-tuple-element.9, f32[2,128]{1,0:T(2,128)S(1)} %add_rsqrt_fusion), kind=kOutput, calls=%fused_computation.159 | convolution fusion | flops 8024211456 | bytes 47515648 | tf_op jit(solution)/shard_map/bsd,dv->bsv/dot_general | solution.py:33
  156.5 17.5 %fusion.124 = (f32[2,128]{1,0:T(2,128)S(1)}, f32[2,128,15296]{1,2,0:T(8,128)}) fusion(bf16[2,128,384]{2,1,0:T(8,128)(2,1)S(1)} %all_gather.6, bf16[384,30592]{1,0:T(8,128)(2,1)} %param.21, s32[]{:T(128)S(6)} %select_n.7), kind=kOutput, calls=%fused_computation.158 | convolution fusion | flops 3011231488 | bytes 27657220 | tf_op jit(solution)/shard_map/bsd,dv->bsv/dot_general | solution.py:33
  174.1 2.5 pmax.7
  176.5 11.3 %fusion.3 = (f32[2,128]{1,0:T(2,128)S(1)}, f32[2,128]{1,0:T(2,128)S(1)}) fusion(f32[2,128,15296]{1,2,0:T(8,128)} %get-tuple-element.49, f32[2,128]{1,0:T(2,128)S(1)} %get-tuple-element.36, f32[2,128,15296]{1,2,0:T(8,128)} %get-tuple-element.47, f32[2,128]{1,0:T(2,128)S(1)} %get-tuple-element.37), kind=kLoop, calls=%fused_computation.8 | loop fusion | flops 15662592 | bytes 31330304 | tf_op jit(solution)/shard_map/reduce_sum | solution.py:243
  187.8 2.5 psum.49
  190.3 13.5 %multiply_convert_fusion = (bf16[2,128,15296]{1,2,0:T(8,128)(2,1)S(1)}, f32[]{:T(128)}) fusion(f32[2,128,15296]{1,2,0:T(8,128)} %get-tuple-element.47, f32[2,128,15296]{1,2,0:T(8,128)} %get-tuple-element.49, f32[2,128]{1,0:T(2,128)S(1)} %get-tuple-element.34, f32[2,128]{1,0:T(2,128)S(1)} %get-tuple-element.35, f32[2,128]{1,0:T(2,128)S(1)} %get-tuple-element.37, ...), kind=kLoop, calls=%fused_computation.3 | loop fusion | flops 43073536 | bytes 39162884 | tf_op jit(solution)/shard_map/convert_element_type | solution.py:249
  203.8 3.1 copy-done.2
  206.8 10.6 %convolution_bitcast_fusion = f32[384,15296]{0,1:T(8,128)} fusion(bf16[2,128,15296]{1,2,0:T(8,128)(2,1)S(1)} %get-tuple-element.32, bf16[2,128,384]{2,1,0:T(8,128)(2,1)S(1)} %all_gather.6), kind=kOutput, calls=%fused_computation.2 | convolution fusion | flops 3007315968 | bytes 31522816 | tf_op jit(solution)/shard_map/bsd,bsv->dv/dot_general | solution.py:33
  217.7 15.7 %fusion.5 = f32[2,128,384]{2,1,0:T(8,128)} fusion(bf16[2,128,15296]{1,2,0:T(8,128)(2,1)} %copy-done.2, bf16[384,30592]{1,0:T(8,128)(2,1)} %param.21, s32[]{:T(128)S(6)} %select_n.7), kind=kOutput, calls=%fused_computation.10 | convolution fusion | flops 3007315968 | bytes 20021252 | tf_op jit(solution)/shard_map/bsv,dv->bsd/dot_general | solution.py:33
  233.5 239.3 %all-reduce.5.cloned.1.call-done = f32[384,15296]{0,1:T(8,128)} async-done(((f32[384,15296]{0,1:T(8,128)}), f32[384,15296]{0,1:T(8,128)}) %all-reduce.5.cloned.1.call-update) | async-done | bytes 23494672 | tf_op jit(solution)/shard_map/psum | solution.py:251
  473.1 1.1 copy-done.3
  474.2 0.9 multiply_reduce_fusion.1
  475.5 1.0 multiply_reduce_fusion.2
  477.3 1.9 pad_maximum_fusion.2
  479.3 1.5 multiply_reduce_fusion.4
  480.9 2.2 fusion.73
  487.0 2.5 pad_maximum_fusion.1
  489.5 2.5 pad_maximum_fusion
  494.7 65.7 %all-reduce = (f32[]{:T(128)}, f32[2,384]{1,0:T(2,128)}) all-reduce(f32[]{:T(128)S(6)} %add.118, f32[2,384]{1,0:T(2,128)S(1)} %pad_maximum_fusion.3), channel_id=1, replica_groups=mesh['dp'=64,'tp'=2] {'dp','tp'}, use_global_device_ids=true, to_apply=%region_13.0 | all-reduce | flops 769 | bytes 6152 | tf_op jit(solution)/shard_map/psum | solution.py:256
  560.4 45.8 %copy.20 = f32[384,30592]{1,0:T(8,128)} copy(f32[384,30592]{0,1:T(8,128)} %all-gather.2.cloned.1.call-done) | data formatting | bytes 93978624
  606.2 114.0 %all-reduce.7.cloned.1.call-done = (f32[2,384,1536]{2,1,0:T(8,128)}, f32[2,1536,384]{2,1,0:T(8,128)}, f32[2,384,1024]{2,1,0:T(8,128)}) async-done(((f32[2,384,1536]{2,1,0:T(8,128)}, f32[2,1536,384]{2,1,0:T(8,128)}, f32[2,384,1024]{2,1,0:T(8,128)}), (f32[2,384,1536]{2,1,0:T(8,128)}, f32[2,1536,384]{2,1,0:T(8,128)}, f32[2,384,1024]{2,1,0:T(8,128)})) %all-reduce.7.cloned.1.call-update) | async-done | bytes 12582928 | tf_op jit(solution)/shard_map/psum | solution.py:255
  720.2 5.0 copy.26
  725.2 2.4 copy.27
  727.6 1.2 copy-done.5
  728.8 1.7 copy.28
  (94 shorter events, 8.8 us)
Async XLA Ops:
  8.0 464.8 %all-reduce.5.cloned.1.call-start = ((), (), s32[]{:S(2)}) async-start(), calls=%async_computation.2 | async-start | bytes 46989312 | tf_op jit(solution)/shard_map/psum | solution.py:251
  8.0 6.8 copy-start.10
  8.1 8.1 %copy-start.26 = (bf16[2,1536,384]{2,1,0:T(8,128)(2,1)S(1)}, bf16[2,1536,384]{2,1,0:T(8,128)(2,1)}, u32[]{:S(2)}) copy-start(bf16[2,1536,384]{2,1,0:T(8,128)(2,1)} %param.18) | copy-start | bytes 7077892
  8.9 5.4 copy-start.18
  9.0 5.4 copy-start.16
  10.5 3.9 copy-start.24
  12.2 5.2 copy-start.6
  12.2 8.2 %copy-start = (bf16[2,64,1024]{2,1,0:T(8,128)(2,1)S(1)}, bf16[2,64,1024]{2,1,0:T(8,128)(2,1)}, u32[]{:S(2)}) copy-start(bf16[2,64,1024]{2,1,0:T(8,128)(2,1)} %x_ref.1) | copy-start | bytes 786436
  12.2 8.2 %copy-start.1 = (f32[32,1024]{1,0:T(8,128)S(1)}, f32[32,1024]{1,0:T(8,128)}, u32[]{:S(2)}) copy-start(f32[32,1024]{1,0:T(8,128)} %gain_ref.1) | copy-start | bytes 393220
  14.3 0.5 copy-start.20
  15.3 0.9 copy-start.8
  16.7 0.7 copy-start.13
  16.7 119.5 %copy-start.22 = (f32[128]{0:T(128)}, f32[128]{0:T(128)S(1)}, u32[]{:S(2)}) copy-start(f32[128]{0:T(128)S(1)} %add_rsqrt_fusion.1) | copy-start | bytes 1540
  203.8 3.1 copy-start.2
  217.4 261.8 %reduce-scatter.2.cloned.1.call-start = ((), (), s32[]{:S(2)}) async-start(), calls=%async_computation.1 | async-start | bytes 589824 | tf_op jit(solution)/shard_map/reduce_scatter | solution.py:253
  233.4 327.0 %all-gather.2.cloned.1.call-start = ((), (), s32[]{:S(2)}) async-start(), calls=%async_computation.3 | async-start | bytes 70483968 | tf_op jit(solution)/shard_map/all_gather | solution.py:251
  472.8 1.4 copy-start.3
  472.8 2.7 copy-start.21
  472.8 247.4 %all-reduce.7.cloned.1.call-start = ((), (), s32[]{:S(2)}) async-start(), calls=%async_computation.4 | async-start | bytes 25165824 | tf_op jit(solution)/shard_map/psum | solution.py:255
  476.5 2.7 copy-start.14
  476.5 2.7 copy-start.23
  477.3 3.6 copy-start.9
  479.2 3.9 copy-start.17
  479.2 3.9 copy-start.11
  480.8 3.2 copy-start.7
  480.8 3.2 copy-start.27
  483.1 1.6 copy-start.15
  483.2 1.6 copy-start.19
  483.2 1.6 copy-start.25
  492.0 2.1 copy-start.12
  720.2 5.0 copy-start.4
  725.2 3.6 copy-start.5
Sparse Core Ops, SparseCore 0:
  217.6 255.1 all-reduce.4
Sparse Core Ops, SparseCore 1:
  233.5 13.0 reduce-scatter.1
  472.9 72.6 all-gather.1
  551.3 168.8 all-reduce.6

commit v2 on v0

v2 whole, which is shorter than its diff:
```python
import functools

import jax
import jax.numpy as jnp
from jax import lax
from jax.experimental import pallas as pl
from jax.experimental.pallas import tpu as pltpu
from jax.sharding import PartitionSpec as P

NORM_EPS = 1e-6
MESH = pl.DeviceIdType.MESH
F32, BF16 = jnp.float32, jnp.bfloat16
DMA = pltpu.SemaphoreType.DMA
IN_VMEM = pl.BlockSpec(memory_space=pltpu.VMEM)
IN_HBM = pl.BlockSpec(memory_space=pl.ANY)
LANES = 128
SUBS = 8
SIDE = 4
MIB = 1 << 20
HERE, RIGHT, FAR, LEFT = range(SIDE)
X, Y, Z = AXES = tuple(range(SIDE - RIGHT))
PARTS = AXES
ORDERS = ((X, Y, Z), (Y, Z, X), (Z, X, Y))
CORES = PAIR = (0, 1)
WAYS = (RIGHT, LEFT)


def chip_coords():
    chip = lax.axis_index('dp')
    return lax.rem(chip, SIDE), lax.rem(chip // SIDE, SIDE), chip // (SIDE * SIDE)


def device(coords, core):
    x, y, z = coords
    return {'dp': (z * SIDE + y) * SIDE + x, 'tp': core}


def moved(coords, axis, step):
    out = list(coords)
    out[axis] = lax.rem(out[axis] + step, SIDE)
    return tuple(out)


def remote(src, dst, send_sem, recv_sem, target):
    return pltpu.make_async_remote_copy(src_ref=src, dst_ref=dst, send_sem=send_sem, recv_sem=recv_sem,
                                        device_id=target, device_id_type=MESH)


def greet(targets):
    barrier = pltpu.get_barrier_semaphore()
    for target in targets:
        pl.semaphore_signal(barrier, device_id=target, device_id_type=MESH)
    pl.semaphore_wait(barrier, len(targets))


def group_targets(coords, core):
    return [device(moved(coords, X, step), abs(core - flip)) for step in range(SIDE) for flip in CORES if step or flip]


def near_targets(coords, core):
    return [device(moved(coords, axis, step), core) for axis in AXES for step in WAYS] + [device(coords, 1 - core)]


def lane_slice(k, width):
    return slice(k * width, k * width + width)


def rms_unit(values):
    inv = lax.rsqrt(jnp.mean(values * values, axis=-1, keepdims=True) + NORM_EPS)
    return values * inv, inv


def rms_back(normed, inv_rms, grad_out):
    return inv_rms * (grad_out - normed * jnp.mean(grad_out * normed, axis=-1, keepdims=True))


GELU_C = 0.7978845608028654
GELU_K = 0.044715


def gelu_act(u):
    half = 0.5 * u
    return half + half * jnp.tanh(u * (GELU_C + (GELU_C * GELU_K) * (u * u)))


def gelu_slope(u):
    sq = u * u
    t = jnp.tanh(u * (GELU_C + (GELU_C * GELU_K) * sq))
    return 0.5 * (1 + t) + (0.5 * u) * (1 - t * t) * (GELU_C + (3 * GELU_C * GELU_K) * sq)


def dot(a, b):
    return jnp.dot(a, b, preferred_element_type=F32)


def dot_right_t(a, b):
    return lax.dot_general(a, b, (((1,), (1,)), ((), ())), preferred_element_type=F32)


def dot_left_t(a, b):
    return lax.dot_general(a, b, (((0,), (0,)), ((), ())), preferred_element_type=F32)


def student_layers(x_ref, gain_ref, up_ref, down_ref):
    residual = x_ref[...].astype(F32)
    unit, inv = rms_unit(residual)
    saved = []
    for j in range(up_ref.shape[0]):
        normed = (unit * gain_ref[j:j + 1, :]).astype(BF16)
        pre = dot(normed, up_ref[j])
        act = gelu_act(pre).astype(BF16)
        residual = residual + dot(act, down_ref[j])
        unit_next, inv_next = rms_unit(residual)
        saved.append((unit, inv, normed, pre, act, unit_next, inv_next))
        unit, inv = unit_next, inv_next
    return saved, unit.astype(BF16)


def teacher_kernel(feat_at, slots_w,
                   x_ref, xs_ref, gs_ref, ups_ref, dns_ref, gain_ref, wup_hbm, wdn_hbm,
                   feat_ref, last_ref, state_ref, group_ref,
                   h, nrm, act, wu, wd, part, got, r_own,
                   usem, dsem, xsend, xrecv, ssem, rsem, gsend, grecv):
    me = lax.axis_index('tp')
    coords = chip_coords()
    peer = device(coords, 1 - me)
    n_layers = gain_ref.shape[0]
    rows, seq_half, d_model = x_ref.shape

    def up_copy(layer, slot):
        return pltpu.make_async_copy(wup_hbm.at[layer], wu.at[slot], usem.at[slot])

    def down_copy(layer, slot):
        return pltpu.make_async_copy(wdn_hbm.at[layer], wd.at[slot], dsem.at[slot])

    for i in range(slots_w):
        up_copy(i, i).start()
        down_copy(i, i).start()
    targets = group_targets(coords, me)
    greet(targets)
    mine = pl.ds(pl.multiple_of(me * seq_half, seq_half), seq_half)
    xcopy = remote(x_ref, h.at[:, mine], xsend, xrecv, peer)
    xcopy.start()
    h[:, mine] = x_ref[...]

    _, head_in = student_layers(xs_ref, gs_ref, ups_ref, dns_ref)
    r_own[...] = head_in
    r_copies = [remote(r_own, group_ref.at[coords[X], me], gsend.at[i], grecv.at[i], target) for i, target in enumerate(targets)]
    for copy in r_copies:
        copy.start()
    group_ref[coords[X], me] = head_in
    xcopy.wait()

    def p_copy(ck, slot):
        return remote(part.at[ck, slot], got.at[ck, slot], ssem.at[ck, slot], rsem.at[ck, slot], peer)

    def update(ck, slot):
        p_copy(ck, slot).wait()
        total = part[ck, slot] + got[ck, slot]
        h[ck] = (h[ck].astype(F32) + total.astype(BF16).astype(F32)).astype(BF16)

    def layer_step(layer, _):
        slot = lax.rem(layer, len(PAIR))
        ws = lax.rem(layer, slots_w)
        for ck in range(rows):
            first, last = ck == 0, ck == rows - 1

            @pl.when(layer > 0)
            def _():
                update(ck, 1 - slot)

            @pl.when((layer == feat_at) & (me == ck))
            def _():
                feat_ref[...] = h[ck]

            unit, _ = rms_unit(h[ck].astype(F32))
            nrm[...] = (unit * gain_ref[pl.ds(layer, 1), :]).astype(BF16)
            if first:
                up_copy(layer, ws).wait()
            act[...] = gelu_act(dot(nrm[...], wu[ws])).astype(BF16)
            if last:
                @pl.when(layer + slots_w < n_layers)
                def _():
                    up_copy(layer + slots_w, ws).start()
            if first:
                down_copy(layer, ws).wait()
            part[ck, slot] = dot(act[...], wd[ws])
            p_copy(ck, slot).start()
            if last:
                @pl.when(layer + slots_w < n_layers)
                def _():
                    down_copy(layer + slots_w, ws).start()
        return 0

    lax.fori_loop(0, n_layers, layer_step, 0)
    for ck in range(rows):
        update(ck, (n_layers - 1) % len(PAIR))

        @pl.when(me == ck)
        def _():
            last_ref[...] = h[ck]

        state_ref[ck] = rms_unit(h[ck].astype(F32))[0].astype(BF16)
    for copy in r_copies:
        copy.wait()


def teacher(x_teach, x_stud, gain_s, w_up_s, w_down_s, gain_t, w_up_t, w_down_t, feat_at, collective_id, slots_w=3):
    n_layers, d_model, d_ff = w_up_t.shape
    rows, seq_half, _ = x_teach.shape
    n_tok = len(PAIR) * seq_half
    n_peers = SIDE * len(PAIR) - 1
    feat = jax.ShapeDtypeStruct((n_tok, d_model), BF16)
    slots = (rows, len(PAIR))
    weights = n_layers * d_model * d_ff
    return pl.pallas_call(
        functools.partial(teacher_kernel, feat_at, slots_w),
        out_shape=(feat, feat, jax.ShapeDtypeStruct((rows, n_tok, d_model), BF16),
                   jax.ShapeDtypeStruct((SIDE, len(PAIR)) + x_stud.shape, BF16)),
        in_specs=[IN_VMEM] * 6 + [IN_HBM] * len(PAIR),
        out_specs=(IN_VMEM,) * SIDE,
        scratch_shapes=[
            pltpu.VMEM((rows, n_tok, d_model), BF16), pltpu.VMEM((n_tok, d_model), BF16), pltpu.VMEM((n_tok, d_ff), BF16),
            pltpu.VMEM((slots_w, d_model, d_ff), BF16), pltpu.VMEM((slots_w, d_ff, d_model), BF16),
            pltpu.VMEM(slots + (n_tok, d_model), F32), pltpu.VMEM(slots + (n_tok, d_model), F32),
            pltpu.VMEM(x_stud.shape, BF16),
            DMA((slots_w,)), DMA((slots_w,)), DMA, DMA, DMA(slots), DMA(slots), DMA((n_peers,)), DMA((n_peers,)),
        ],
        compiler_params=pltpu.CompilerParams(collective_id=collective_id, has_side_effects=True, vmem_limit_bytes=52 * MIB),
        cost_estimate=pl.CostEstimate(flops=SIDE * rows * n_tok * weights, bytes_accessed=SIDE * weights, transcendentals=0),
        name='teacher',
    )(x_teach, x_stud, gain_s, w_up_s, w_down_s, gain_t, w_up_t, w_down_t)


NEG = -1e38
MAX_T, SUM_T, MAX_S, SUM_S = STATS = range(SIDE)
TEACH, STUD = PAIR


def heads_kernel(kl_coef, chunk,
                 t_ref, r_ref, ht_hbm, hs_hbm,
                 dw_hbm, dx_ref, kl_ref,
                 tg, rt, ht, hs, zt, zs, mx, sm, st_send, st_all, lcol, grad, dx, px, ds, dr,
                 ht_sem, hs_sem, ring_send, ring_recv, peer_send, peer_recv, st_send_sem, st_recv_sem, dx_send, dx_recv, out_sem):
    coords = chip_coords()
    x = coords[X]
    core = lax.axis_index('tp')
    peer = device(coords, 1 - core)
    rows, n_tok, d_model = t_ref.shape
    d_stud, cols = hs.shape
    n_tiles = cols // LANES
    blk = rows * n_tok
    n_all = SIDE * blk
    half_tile = LANES // 2
    last_x = SIDE - 1

    first_tile = n_tiles * x + core * (n_tiles * SIDE - 1)
    hs_copy = pltpu.make_async_copy(hs_hbm.at[:, pl.ds(pl.multiple_of(first_tile * LANES, LANES), cols)], hs, hs_sem)
    hs_copy.start()
    cut_low = (core == 1) & (x == 0)
    cut_high = (core == 0) & (x == last_x)

    def ht_copy(src, dst, n):
        return pltpu.make_async_copy(ht_hbm.at[pl.ds(src, n)], ht.at[pl.ds(dst, n)], ht_sem)

    def each_ht(act):
        @pl.when(jnp.logical_not(cut_low | cut_high))
        def _():
            act(ht_copy(pl.multiple_of(cols * x - half_tile * core, half_tile), 0, cols))

        @pl.when(cut_low)
        def _():
            act(ht_copy(0, half_tile, cols - half_tile))

        @pl.when(cut_high)
        def _():
            act(ht_copy(last_x * cols, 0, cols - half_tile))

    each_ht(lambda copy: copy.start())
    targets = group_targets(coords, core)
    greet(targets)

    far_rows = n_tok // 2

    def at(step):
        return lax.rem(x + step, SIDE)

    def ring(k, src, dst, step):
        return remote(src, dst, ring_send.at[k], ring_recv.at[k], device(moved(coords, X, step), core))

    def onward(k, step, way):
        piece = tg.at[at(step), core, pl.ds(k * far_rows, far_rows)]
        return ring(k + len(PAIR), piece, piece, way)

    def first(k, step, way):
        return ring(k, t_ref.at[core], tg.at[at(step), core], way)

    def across(step, side):
        piece = tg.at[at(step), side]
        return remote(piece, piece, peer_send.at[step - 1], peer_recv.at[step - 1], peer)

    opposite = (LEFT, RIGHT)
    for k, way in enumerate(WAYS):
        first(k, HERE, way).start()
    tg[x] = t_ref[...]
    rt[...] = r_ref[...].T
    lane = lax.broadcasted_iota(jnp.int32, (blk, LANES), 1)
    low = jnp.where(cut_low, half_tile, 0)
    high = jnp.where(cut_high, half_tile, LANES)

    def finish(kind, b, ref):
        head, tail = lane_slice(0, LANES), lane_slice(n_tiles - 1, LANES)
        ref[b, :, head] = jnp.where(lane >= low, ref[b, :, head], NEG)
        ref[b, :, tail] = jnp.where(lane < high, ref[b, :, tail], NEG)
        tiles = [lane_slice(k, LANES) for k in range(n_tiles)]
        peak = functools.reduce(jnp.maximum, [ref[b, :, t] for t in tiles])
        mx[kind, b] = peak
        sm[kind, b] = functools.reduce(jnp.add, [jnp.exp(ref[b, :, t] - peak) for t in tiles])

    def tokens(b):
        return pl.ds(pl.multiple_of(b * blk, blk), blk)

    def student_logits(b, _):
        zs[b] = dot(r_ref[tokens(b), :], hs[...])
        finish(STUD, b, zs)
        return 0

    hs_copy.wait()
    lax.fori_loop(0, FAR, student_logits, 0)
    for k, way in enumerate(WAYS):
        first(k, opposite[k], way).wait_recv()
        onward(k, opposite[k], way).start()
        across(opposite[k], core).start()
    lax.fori_loop(FAR, SIDE, student_logits, 0)
    for k, way in enumerate(WAYS):
        onward(k, FAR, way).wait_recv()
    across(FAR, core).start()
    each_ht(lambda copy: copy.wait())

    def teacher_logits(i, _):
        for step, turn in ((RIGHT, 1), (LEFT, 2), (FAR, 3)):
            @pl.when(i == turn)
            def _():
                across(step, 1 - core).wait_recv()

        b = at(jnp.where(i < FAR, i, SIDE + 1 - i))
        zt[b] = dot_right_t(tg[b].reshape(blk, d_model), ht[...])
        finish(TEACH, b, zt)
        return 0

    lax.fori_loop(0, SIDE, teacher_logits, 0)

    def merge(b, _):
        out = jnp.zeros((blk, LANES), F32)
        for kind in PAIR:
            peak = jnp.max(mx[kind, b], axis=-1, keepdims=True)
            total = jnp.sum(sm[kind, b] * jnp.exp(mx[kind, b] - peak), axis=-1, keepdims=True)
            out = jnp.where(lane == 2 * kind, peak, jnp.where(lane == 2 * kind + 1, total, out))
        st_send[:, tokens(b)] = out.T[:SUBS, :]
        return 0

    lax.fori_loop(0, SIDE, merge, 0)
    n_peers = len(targets)
    stats = [remote(st_send, st_all.at[i], st_send_sem.at[i], st_recv_sem.at[i], target) for i, target in enumerate(targets)]
    for copy in stats:
        copy.start()
    st_all[n_peers] = st_send[...]
    for copy in stats:
        copy.wait()
    sub = lax.broadcasted_iota(jnp.int32, (LANES, n_all), 0)
    both = jnp.zeros((LANES, n_all), F32)
    for kind in PAIR:
        peaks, totals = st_all[:, 2 * kind, :], st_all[:, 2 * kind + 1, :]
        peak = jnp.max(peaks, axis=0, keepdims=True)
        norm = peak + jnp.log(jnp.sum(totals * jnp.exp(peaks - peak), axis=0, keepdims=True))
        both = jnp.where(sub == kind, norm, both)
    lcol[...] = both.T
    kl_ref[...] = jnp.zeros_like(kl_ref)
    dx[...] = jnp.zeros_like(dx)

    def grad_step(j, _):
        lanes = pl.ds(pl.multiple_of(j * chunk, LANES), chunk)

        def block(b, _):
            tok = tokens(b)
            log_pt = zt[b, :, lanes] - lcol[tok, TEACH:TEACH + 1]
            log_ps = zs[b, :, lanes] - lcol[tok, STUD:STUD + 1]
            pt = jnp.exp(log_pt)
            grad[tok, :] = (kl_coef * (jnp.exp(log_ps) - pt)).astype(BF16)
            kl = pt * (log_pt - log_ps)
            kl = functools.reduce(jnp.add, [kl[:, lane_slice(k, LANES)] for k in range(chunk // LANES)])
            kl_ref[...] += functools.reduce(jnp.add, [kl[lane_slice(k, SUBS)] for k in range(blk // SUBS)])
            return 0

        lax.fori_loop(0, SIDE, block, 0)
        dw = dot(rt[...], grad[...])
        zt[0, :, lanes] = dw[:blk]
        zt[1, :d_stud - blk, lanes] = dw[blk:]
        dx[...] += dot_right_t(grad[...], hs[:, lanes])
        return 0

    lax.fori_loop(0, cols // chunk, grad_step, 0)
    outs = [pltpu.make_async_copy(zt.at[k, pl.ds(0, n)], dw_hbm.at[pl.ds(k * blk, n)], out_sem.at[k])
            for k, n in enumerate((blk, d_stud - blk))]
    for copy in outs:
        copy.start()

    for s in range(SIDE):
        for c in CORES:
            ds[c, s] = dx[lane_slice(2 * s + c, n_tok)]
    swap = remote(ds.at[1 - core], px, dx_send.at[HERE], dx_recv.at[HERE], peer)
    swap.start()
    swap.wait()
    ds[core] = ds[core] + px[...]
    passes = [remote(ds.at[core, at(step)], dr.at[step - 1], dx_send.at[step], dx_recv.at[step], device(moved(coords, X, step), core))
              for step in (RIGHT, FAR, LEFT)]
    for copy in passes:
        copy.start()
    for copy in passes:
        copy.wait()
    dx_ref[...] = functools.reduce(jnp.add, [dr[i] for i in range(last_x)], ds[core, x])
    for k, way in enumerate(WAYS):
        first(k, HERE, way).wait_send()
        onward(k, opposite[k], way).wait_send()
    for step in (RIGHT, FAR, LEFT):
        across(step, core).wait_send()
    for copy in outs:
        copy.wait()


def heads(states, stud_all, head_t, head_s, kl_coef, collective_id, chunk=768):
    rows, n_tok, d_model = states.shape
    n_all, d_stud = stud_all.shape
    cols = -(-head_t.shape[1] // (LANES * SIDE)) * LANES
    blk = rows * n_tok
    n_peers = SIDE * len(PAIR) - 1
    v = pltpu.VMEM
    hops = (SIDE - 1,)
    return pl.pallas_call(
        functools.partial(heads_kernel, kl_coef, chunk),
        out_shape=(jax.ShapeDtypeStruct((d_stud, cols), F32), jax.ShapeDtypeStruct((n_tok, d_stud), F32),
                   jax.ShapeDtypeStruct((SUBS, LANES), F32)),
        in_specs=[IN_VMEM, IN_VMEM, IN_HBM, IN_HBM],
        out_specs=(IN_HBM, IN_VMEM, IN_VMEM),
        scratch_shapes=[
            v((SIDE, rows, n_tok, d_model), BF16), v((d_stud, n_all), BF16), v((cols, d_model), BF16), v((d_stud, cols), BF16),
            v((SIDE, blk, cols), F32), v((SIDE, blk, cols), F32),
            v((len(PAIR), SIDE, blk, LANES), F32), v((len(PAIR), SIDE, blk, LANES), F32),
            v((SUBS, n_all), F32), v((n_peers + 1, SUBS, n_all), F32), v((n_all, LANES), F32),
            v((n_all, chunk), BF16), v((n_all, d_stud), F32), v((SIDE, n_tok, d_stud), F32),
            v((len(PAIR), SIDE, n_tok, d_stud), F32), v(hops + (n_tok, d_stud), F32),
            DMA, DMA, DMA((SIDE,)), DMA((SIDE,)), DMA(hops), DMA(hops), DMA((n_peers,)), DMA((n_peers,)),
            DMA((SIDE,)), DMA((SIDE,)), DMA((len(PAIR),)),
        ],
        compiler_params=pltpu.CompilerParams(collective_id=collective_id, has_side_effects=True, vmem_limit_bytes=63 * MIB),
        cost_estimate=pl.CostEstimate(flops=d_model * n_all * cols, bytes_accessed=d_model * cols, transcendentals=0),
        name='heads',
    )(states, stud_all, head_t.T, head_s)


class RingSum:
    def __init__(self, coords, core, src, dims, order, lanes, bufs):
        self.coords, self.core, self.order, self.lanes = coords, core, order, lanes
        self.phases = []
        for axis, (half, full, mid, send, recv) in zip(order, bufs):
            self.phases.append((src, dims, axis, half, full, mid, send, recv))
            src, dims = mid, tuple(d for d in dims if d != axis)

    @staticmethod
    def shapes(dims, order, rows, width):
        out = []
        for _ in order:
            dims = dims[1:]
            lead = (SIDE,) * len(dims)
            part = (SIDE // 2,) + lead[1:] + (rows, width) if lead else (rows, -(-width // (2 * LANES)) * LANES)
            out += [pltpu.VMEM(PAIR_DIM + part, F32), pltpu.VMEM(PAIR_DIM + lead + (rows, width), F32),
                    pltpu.VMEM(lead + (rows, width), F32), DMA((3 * len(PAIR),)), DMA((3 * len(PAIR),))]
        return out

    def place(self, axis, step):
        return lax.rem(self.coords[axis] + step, SIDE)

    def split(self, k, side):
        _, dims, _, half, full, _, _, _ = self.phases[k]
        width, cut = full.shape[-1], half.shape[-1]
        if len(dims) > 1:
            return (pl.ds(side * (SIDE // 2), SIDE // 2),) + (slice(None),) * (len(dims) - 2), (0, width)
        return (), ((cut, width - cut) if side else (0, cut))

    def pick(self, k, at, side):
        src, dims, axis = self.phases[k][:3]
        lead, (lo, n) = ((slice(None),) * (len(dims) - 1), (0, self.phases[k][4].shape[-1])) if side is None else self.split(k, side)
        lead = list(lead)
        lead.insert(dims.index(axis), at)
        base = self.lanes if k == 0 else 0
        return src, tuple(lead) + (slice(None), pl.ds(base + lo, n))

    def copy(self, k, turn, d):
        _, _, axis, half, full, _, send, recv = self.phases[k]
        way = WAYS[d]
        i = turn * len(PAIR) + d
        side = d if turn != 1 else 1 - d
        lead, (lo, n) = self.split(k, side)
        window = (slice(None), pl.ds(lo, n))
        if turn == 0:
            ref, idx = self.pick(k, self.place(axis, FAR), side)
            src, dst = ref.at[idx], half.at[d, ..., pl.ds(0, n)]
        elif turn == 1:
            ref, idx = self.pick(k, self.place(axis, way), side)
            src, dst = ref.at[idx], full.at[(d,) + lead + window]
        else:
            src, dst = half.at[d, ..., pl.ds(0, n)], full.at[(d,) + lead + window]
        return remote(src, dst, send.at[i], recv.at[i], device(moved(self.coords, axis, way), self.core))

    def start(self, k):
        for turn in PAIR:
            for d in PAIR:
                self.copy(k, turn, d).start()

    def middle(self, k):
        _, _, axis, half, _, _, _, _ = self.phases[k]
        for d in PAIR:
            self.copy(k, 0, d).wait_recv()
            ref, idx = self.pick(k, self.place(axis, WAYS[d]), d)
            n = self.split(k, d)[1][1]
            half[d, ..., :n] = half[d, ..., :n] + ref[idx]
            self.copy(k, len(PAIR), d).start()

    def finish(self, k):
        _, _, axis, _, full, mid, _, _ = self.phases[k]
        for d in PAIR:
            for turn in (1, len(PAIR)):
                self.copy(k, turn, d).wait_recv()
        ref, idx = self.pick(k, self.coords[axis], None)
        mid[...] = ref[idx] + full[0] + full[1]

    def drain(self):
        for k in range(len(self.order)):
            for turn in range(3):
                for d in PAIR:
                    self.copy(k, turn, d).wait_send()


PAIR_DIM = (len(PAIR),)


def small_places(n_feat, d_in, d_mid, d_teach):
    groups_up = d_in // SUBS
    yz = SIDE * SIDE
    per_up = n_feat * groups_up // yz
    lanes_u, lanes_p = d_mid // SIDE, d_teach // SIDE
    per_p = groups_up // yz
    span = per_up // per_p * lanes_u + lanes_p
    return groups_up, yz, per_up, lanes_u, lanes_p, per_p, span


def reduce_kernel(feat_coef, kl_coef, small_parts,
                  dw, dx_ref, feat_a, feat_b, xs_ref, gs_ref, ups_ref, dns_ref, proj_ref, kl_ref,
                  own, small, got, swap_send, swap_recv, *bufs):
    coords = chip_coords()
    core = lax.axis_index('tp')
    peer = device(coords, 1 - core)
    greet(near_targets(coords, core))
    cols = dw.shape[-1]
    bufs = list(bufs)

    def take(n):
        out = [tuple(bufs[5 * i:5 * i + 5]) for i in range(n)]
        del bufs[:5 * n]
        return out

    head_jobs = [RingSum(coords, core, dw, (Y, Z), order, k * (cols // 2), take(2)) for k, order in enumerate(((Y, Z), (Z, Y)))]
    for job in head_jobs:
        job.start(0)

    saved, _ = student_layers(xs_ref, gs_ref, ups_ref, dns_ref)
    feats = (feat_a, feat_b)
    n_feat, d_in, d_mid = ups_ref.shape
    groups, yz, per_up, lanes_u, lanes_p, per_p, span = small_places(n_feat, d_in, d_mid, proj_ref.shape[-1])
    two = per_up // per_p
    err_rows = jnp.zeros((SUBS, LANES), F32)
    resid_grad = None
    gain_rows = []

    def put(keep, chip_x, group, per, base, lanes, value):
        block, g = divmod(group, per)
        y, z = divmod(block, SIDE)
        part, q = divmod(g, per // per_p)
        small[keep, chip_x, y, z, :, part * span + base + q * lanes:part * span + base + q * lanes + lanes] = value

    for j in reversed(range(n_feat)):
        unit, inv, normed, pre, act, unit_next, inv_next = saved[j]
        proj_in = unit_next.astype(BF16)
        err = dot(proj_in, proj_ref[j]) - feats[j][...].astype(F32)
        sq = err * err
        sq = functools.reduce(jnp.add, [sq[:, lane_slice(k, LANES)] for k in range(sq.shape[1] // LANES)])
        err_rows = err_rows + functools.reduce(jnp.add, [sq[lane_slice(k, SUBS)] for k in range(sq.shape[0] // SUBS)])
        err_grad = ((2 * feat_coef) * err).astype(BF16)
        g_proj = dot_left_t(proj_in, err_grad)
        for i in range(groups):
            for cx in range(SIDE):
                put(j, cx, i, per_p, two * lanes_u, lanes_p, g_proj[lane_slice(i, SUBS), lane_slice(cx, lanes_p)])
        out_grad = dot_right_t(err_grad, proj_ref[j])
        if resid_grad is None:
            resid_grad = rms_back(unit_next, inv_next, out_grad + dx_ref[...])
        else:
            resid_grad = resid_grad + rms_back(unit_next, inv_next, out_grad)
        resid_bf = resid_grad.astype(BF16)
        g_down = dot_left_t(act, resid_bf)
        n_down = d_mid // SUBS
        for i in range(n_down):
            cx, rest = divmod(j * n_down + i, n_feat * n_down // SIDE)
            put(1, cx, rest, per_up, 0, lanes_u, g_down[lane_slice(i, SUBS), :])
        pre_grad = (gelu_slope(pre) * dot_right_t(resid_bf, dns_ref[j])).astype(BF16)
        g_up = dot_left_t(normed, pre_grad)
        for i in range(groups):
            for cx in range(SIDE):
                put(0, cx, j * groups + i, per_up, 0, lanes_u, g_up[lane_slice(i, SUBS), lane_slice(cx, lanes_u)])
        norm_grad = dot_right_t(pre_grad, ups_ref[j])
        g_gain = jnp.sum(norm_grad * unit, axis=0, keepdims=True)
        gain_rows = [g_gain[:, lane_slice(k, LANES)] for k in range(d_in // LANES)] + gain_rows
        if j > 0:
            resid_grad = resid_grad + rms_back(unit, inv, norm_grad * gs_ref[j:j + 1, :])

    swaps = [remote(small.at[1 - core, cx], got.at[cx], swap_send.at[cx], swap_recv.at[cx], peer) for cx in range(SIDE)]
    for copy in swaps:
        copy.start()
    for job in head_jobs:
        job.middle(0)
    for cx, copy in enumerate(swaps):
        copy.wait()
        got[cx] = got[cx] + small[core, cx]
    lo = 0
    small_jobs = []
    for order, width in zip(ORDERS, small_parts):
        small_jobs.append(RingSum(coords, core, got, AXES, order, lo, take(3)))
        lo += width
    for job in small_jobs:
        job.start(0)
    for job in head_jobs:
        job.finish(0)
        job.start(1)
    for job in small_jobs:
        job.middle(0)
    for job in head_jobs:
        job.middle(1)
    for job in small_jobs:
        job.finish(0)
        job.start(1)
    for job in head_jobs:
        job.finish(1)
    for job in small_jobs:
        job.middle(1)
    for job in small_jobs:
        job.finish(1)
        job.start(2)
    for job in small_jobs:
        job.middle(2)
    for job in small_jobs:
        job.finish(2)
    for p in PARTS:
        for k, job in enumerate(head_jobs):
            own[p, :, lane_slice(k, cols // 2)] = job.phases[-1][5][lane_slice(p, SUBS), :]
    pieces = [(order_i, t) for order_i, width in enumerate(small_parts) for t in range(width // LANES)]
    for n, (which, t) in enumerate(pieces):
        p, at = divmod(n * LANES, span)
        own[p, :, cols + at:cols + at + LANES] = small_jobs[which].phases[-1][5][:, lane_slice(t, LANES)]
    loss_row = jnp.sum(feat_coef * err_rows + kl_coef * kl_ref[...], axis=0, keepdims=True)
    for p in PARTS:
        own[p, :, cols + span:] = jnp.zeros((SUBS, LANES), F32)
    for i, row in enumerate(gain_rows + [loss_row]):
        own[0, i:i + 1, cols + span:] = row
    for job in head_jobs + small_jobs:
        job.drain()


def reduce_grads(dw, dx, feats, x_stud, gain_s, w_up_s, w_down_s, proj_s, kl_tiles, feat_coef, kl_coef, collective_id,
                 small_parts=(2048, 512, 512)):
    rows, cols = dw.shape[2:]
    span = sum(small_parts) // len(PARTS)
    width = cols // 2
    scratch = [pltpu.VMEM((len(PAIR), SIDE, SIDE, SIDE, SUBS, sum(small_parts)), F32),
               pltpu.VMEM((SIDE, SIDE, SIDE, SUBS, sum(small_parts)), F32), DMA((SIDE,)), DMA((SIDE,))]
    for _ in PAIR:
        scratch += RingSum.shapes((Y, Z), (Y, Z), rows, width)
    for part in small_parts:
        scratch += RingSum.shapes(AXES, AXES, SUBS, part)
    return pl.pallas_call(
        functools.partial(reduce_kernel, feat_coef, kl_coef, small_parts),
        out_shape=jax.ShapeDtypeStruct((len(PARTS), SUBS, cols + span + LANES), F32),
        in_specs=[IN_VMEM] * 10,
        out_specs=IN_VMEM,
        scratch_shapes=scratch,
        compiler_params=pltpu.CompilerParams(collective_id=collective_id, has_side_effects=True, vmem_limit_bytes=62 * MIB),
        cost_estimate=pl.CostEstimate(flops=MIB * MIB, bytes_accessed=dw.size, transcendentals=0),
        name='reduce',
    )(dw, dx, *feats, x_stud, gain_s, w_up_s, w_down_s, proj_s, kl_tiles)


ALL = pl.ds(0, SIDE)


def gather_kernel(cut, own_ref, full, own_sem, send_sem, recv_sem, peer_send, peer_recv):
    coords = chip_coords()
    core = lax.axis_index('tp')
    peer = device(coords, 1 - core)
    width = own_ref.shape[-1]
    widths = (width, width - LANES, width - LANES)
    here = [pltpu.make_async_copy(own_ref.at[p], full.at[(core,) + coords + (p,)], own_sem.at[p]) for p in PARTS]
    for copy in here:
        copy.start()
    greet(near_targets(coords, core))
    whole, low, high = range(3)

    def lanes(part, span):
        return pl.ds(cut if span == high else 0, (widths[part], cut, widths[part] - cut)[span])

    def at_of(part, phase, step):
        return lax.rem(coords[ORDERS[part][phase]] + step, SIDE)

    def block(part, phase, step, span):
        idx = list(coords)
        for k, axis in enumerate(ORDERS[part][:phase + 1]):
            idx[axis] = ALL if k < phase else at_of(part, phase, step)
        return full.at[(core,) + tuple(idx) + (part, slice(None), lanes(part, span))]

    def ring(part, phase, slot, step, span):
        dst = block(part, phase, step, span)
        src = own_ref.at[part, :, lanes(part, span)] if phase == 0 and step == HERE else dst
        return remote(src, dst, send_sem.at[part, phase, slot], recv_sem.at[part, phase, slot],
                      device(moved(coords, ORDERS[part][phase], WAYS[slot % 2]), core))

    def first(part, phase, d, step):
        return ring(part, phase, d, step, whole)

    def onward(part, phase, d, step):
        return ring(part, phase, d + 2, step, (low, high)[d])

    def across(part, phase, step):
        src = block(part, phase, step, whole)
        return remote(src, src, peer_send.at[part, phase, step], peer_recv.at[part, phase, step], peer)

    def own_across(part):
        dst = block(part, 0, HERE, whole)
        return remote(own_ref.at[part, :, lanes(part, whole)], dst, peer_send.at[part, 0, HERE], peer_recv.at[part, 0, HERE], peer)

    source = (LEFT, RIGHT)
    for part in PARTS:
        for d in PAIR:
            first(part, 0, d, HERE).start()
        own_across(part).start()
    for phase in AXES:
        for part in PARTS:
            for d in PAIR:
                first(part, phase, d, source[d]).wait_recv()
                onward(part, phase, d, source[d]).start()
                across(part, phase, source[d]).start()
        for part in PARTS:
            for d in PAIR:
                onward(part, phase, d, FAR).wait_recv()
            if phase == 0:
                here[part].wait()
            if phase < AXES[-1]:
                for d in PAIR:
                    first(part, phase + 1, d, HERE).start()
            across(part, phase, FAR).start()
    for part in PARTS:
        for phase in AXES:
            for d in PAIR:
                first(part, phase, d, HERE).wait_send()
                onward(part, phase, d, source[d]).wait_send()
            for step in (LEFT, RIGHT, FAR):
                across(part, phase, step).wait()
        own_across(part).wait()


def gather_blocks(own, cut, collective_id):
    sems = DMA((len(PARTS), len(AXES), SIDE))
    return pl.pallas_call(
        functools.partial(gather_kernel, cut),
        out_shape=jax.ShapeDtypeStruct((len(PAIR), SIDE, SIDE, SIDE) + own.shape, F32),
        in_specs=[IN_VMEM],
        out_specs=IN_HBM,
        scratch_shapes=[DMA((len(PARTS),)), sems, sems, sems, sems],
        compiler_params=pltpu.CompilerParams(collective_id=collective_id, has_side_effects=True),
        cost_estimate=pl.CostEstimate(flops=MIB * MIB, bytes_accessed=SIDE * LANES * own.size, transcendentals=0),
        name='gather',
    )(own)


N_BUF = 6
N_LATE = N_BUF // 2


def place_kernel(n_head, lanes_u, lanes_p,
                 full, head, up, down, proj, total,
                 bufs, edge, wide, narrow, tiles,
                 in_sem, out_sem, edge_sem, wide_in, wide_out, narrow_in, narrow_out, tile_sem):
    last_x = SIDE - 1
    per = wide.shape[3]
    copy = pltpu.make_async_copy
    narrow_at = n_head + per * lanes_u
    tile_copy = copy(full.at[:, :, :, 0, :, pl.ds(narrow_at + lanes_p, LANES)], tiles, tile_sem)
    tile_copy.start()
    owners = [(c, x) for c in CORES for x in range(SIDE)]
    jobs = [owner + (s,) for owner in owners for s in range(SIDE)]

    def fetch(i):
        c, x, s = jobs[i]
        slot = i % N_BUF
        blocks = pl.ds(s * SIDE, SIDE)
        out = [copy(full.at[c, x, blocks, :, :, pl.ds(0, n_head)], bufs.at[slot], in_sem.at[slot])]
        if (c, x) == PAIR[::-1]:
            out.append(copy(full.at[0, last_x, blocks, :, :, pl.ds(n_head - LANES, LANES)], edge.at[slot], edge_sem.at[slot]))
        return out

    def put(i):
        c, x, s = jobs[i]
        slot = i % N_BUF
        n = n_head - LANES if (c, x) == (0, last_x) else n_head
        at = (c * SIDE + x) * n_head - c * LANES
        return copy(bufs.at[slot, :, :, :, pl.ds(0, n)], head.at[pl.ds(s * SIDE, SIDE), :, :, pl.ds(at, n)], out_sem.at[slot])

    def small_fetch(i):
        c, x = owners[i]
        slot = i % 2
        out = [copy(full.at[c, x, :, :, :, pl.ds(n_head + q * lanes_u, lanes_u)], wide.at[slot, :, :, q], wide_in.at[slot, q])
               for q in range(per)]
        return out + [copy(full.at[c, x, :, :, :, pl.ds(narrow_at, lanes_p)], narrow.at[slot], narrow_in.at[slot])]

    def small_put(i):
        c, x = owners[i]
        slot = i % 2
        dst = down.at[x] if c else up.at[:, :, :, :, pl.ds(x * lanes_u, lanes_u)]
        return [copy(wide.at[slot], dst, wide_out.at[slot]),
                copy(narrow.at[slot], proj.at[c, :, :, :, pl.ds(x * lanes_p, lanes_p)], narrow_out.at[slot])]

    def each(copies, act):
        for one in copies:
            act(one)

    start, wait = (lambda one: one.start()), (lambda one: one.wait())
    for i in range(N_LATE):
        each(fetch(i), start)
    each(small_fetch(0), start)
    for i in range(len(jobs)):
        nxt = i + N_LATE
        if nxt < len(jobs):
            if nxt >= N_BUF:
                wait(put(nxt - N_BUF))
            each(fetch(nxt), start)
        each(fetch(i), wait)
        if jobs[i][:2] == PAIR[::-1]:
            slot = i % N_BUF
            bufs[slot, :, :, :, :LANES] = bufs[slot, :, :, :, :LANES] + edge[slot]
        start(put(i))
        if i % SIDE == SIDE - 1:
            k = i // SIDE
            each(small_fetch(k), wait)
            each(small_put(k), start)
            if k:
                each(small_put(k - 1), wait)
            if k + 1 < len(owners):
                each(small_fetch(k + 1), start)
    tile_copy.wait()
    sums = jnp.sum(tiles[...].reshape(-1, SUBS, LANES), axis=0)
    total[...] = sums
    for i in range(len(jobs) - N_BUF, len(jobs)):
        wait(put(i))
    each(small_put(len(owners) - 1), wait)


def place_blocks(full, n_head, lanes_u, lanes_p, vocab):
    _, _, n_yz, n_part, subs, _ = full.shape
    per = len(PAIR)
    v = pltpu.VMEM
    pair = (len(PAIR),)
    shapes = ((n_yz, n_part, subs, vocab), (n_yz, n_part, per, subs, SIDE * lanes_u), (SIDE, n_yz, n_part, per, subs, lanes_u),
              pair + (n_yz, n_part, subs, SIDE * lanes_p), (subs, LANES))
    return pl.pallas_call(
        functools.partial(place_kernel, n_head, lanes_u, lanes_p),
        out_shape=tuple(jax.ShapeDtypeStruct(s, F32) for s in shapes),
        in_specs=[IN_HBM],
        out_specs=(IN_HBM,) * SIDE + (IN_VMEM,),
        scratch_shapes=[v((N_BUF, SIDE, n_part, subs, n_head), F32), v((N_BUF, SIDE, n_part, subs, LANES), F32),
                        v(pair + (n_yz, n_part, per, subs, lanes_u), F32), v(pair + (n_yz, n_part, subs, lanes_p), F32),
                        v(pair + (SIDE, n_yz, subs, LANES), F32),
                        DMA((N_BUF,)), DMA((N_BUF,)), DMA((N_BUF,)), DMA(pair + (per,)), DMA(pair), DMA(pair), DMA(pair), DMA],
        compiler_params=pltpu.CompilerParams(has_side_effects=True, vmem_limit_bytes=56 * MIB),
        name='place',
    )(full)


def solution(mesh):
    n_dev = mesh.shape['dp'] * mesh.shape['tp']

    def local_step(x_teach, x_stud, w_up_t, w_down_t, gain_t, head_t, w_up_s, w_down_s, gain_s, proj_s, head_s):
        n_feat, d_in, d_mid = w_up_s.shape
        d_teach = proj_s.shape[-1]
        n_tokens = x_stud.shape[0] * x_stud.shape[1] * n_dev
        feat_coef = 1.0 / (n_feat * n_tokens * d_teach)
        kl_coef = 1.0 / n_tokens
        xs = x_stud[0]
        feat_one, feat_two, states, stud_all = teacher(x_teach, xs, gain_s, w_up_s, w_down_s, gain_t, w_up_t, w_down_t,
                                                       w_up_t.shape[0] // n_feat, 0)
        head_part, head_in_grad, kl_tiles = heads(states, stud_all.reshape(-1, d_in), head_t, head_s, kl_coef, 1)
        cols = head_part.shape[1]
        own = reduce_grads(head_part.reshape(SIDE, SIDE, -1, cols), head_in_grad, (feat_one, feat_two), xs, gain_s, w_up_s, w_down_s,
                           proj_s, kl_tiles, feat_coef, kl_coef, 2)
        blocks = gather_blocks(own, 20 * LANES, 3)
        blocks = blocks.reshape(blocks.shape[:2] + (SIDE * SIDE,) + blocks.shape[-3:])
        head_grad, up, down, proj, total = place_blocks(blocks, cols, d_mid // SIDE, d_teach // SIDE, head_s.shape[1])
        n_gain = n_feat * d_in // LANES
        return (jnp.sum(total[n_gain]), up.reshape(w_up_s.shape), down.reshape(w_down_s.shape), total[:n_gain].reshape(gain_s.shape),
                proj.reshape(proj_s.shape), head_grad.reshape(head_s.shape))

    in_specs = (P('dp', 'tp', None), P(('dp', 'tp'), None, None), P(None, None, 'tp'), P(None, 'tp', None),
                P(), P(None, 'tp'), P(), P(), P(), P(), P())
    out_specs = (P(), P(), P(), P(), P(), P())
    return jax.shard_map(local_step, mesh=mesh, in_specs=in_specs, out_specs=out_specs, check_vma=False)
```

time: 1380 us -> 448 us (0.32)
  waiting for transfers between devices: 744 us -> 0 us
  Pallas kernels: 0 us -> 439 us
  matrix products: 307 us -> 0 us
  blocking collectives: 157 us -> 0 us
  other arithmetic: 77.3 us -> 1.29 us
  local copies, waits for them, and re-layouts: 63.8 us -> 6.88 us
  between operations: 17.5 us -> 0.7 us
    pallas_call x0 -> x5, Pallas kernels: none -> 439 us  [the longest x1 132 us: gather_blocks(): pl.pallas_call(functools.partial(gather_kernel, cut), out_shape=jax.Shape...]
    reduce_scatter x33 -> x0, waiting for transfers between devices: 384 us -> none  [the longest x32 384 us: local_step(): lax.psum_scatter(partial_out, 'tp', scatter_dimension=1, tiled=True)]
    psum x2 -> x0, waiting for transfers between devices: 359 us -> none  [the longest x1 238 us: local_step(): lax.psum(head_part, 'dp')]
    dot_general x54 -> x0, matrix products: 307 us -> none  [mat_mul(): jnp.einsum(subscripts, lhs_arr, rhs_arr, preferred_element_type=jnp.float32)]
    all_gather x34 -> x0, blocking collectives: 77.3 us -> none  [the longest x32 73 us: local_step(): gathered = lax.all_gather(normed, 'tp', axis=1, tiled=True)]
    psum x2 -> x0, blocking collectives: 67.4 us -> none  [the longest x1 64.7 us: local_step(): lax.psum(feat_coef * err_total + kl_coef * kl_local, ('dp', 'tp'))]
    unnamed x52 -> x14, local copies, waits for them, and re-layouts: 62 us -> 5.61 us
    reduce_sum x35 -> x1, other arithmetic: 50.7 us -> 1.29 us  [local_step(): jnp.sum(total[n_gain])]
  transfers between devices with their start and end apart: 36 -> 0, of which waited for: 33 -> 0; matrix products, arithmetic and copies ran while one was open for 8% -> 0% of each run, Pallas kernels for 0% -> 0%
where the time goes in v2:
time: 448 us; the launch traced here: 447 us
  Pallas kernels  439 us (98%)
  local copies, waits for them, and re-layouts  6.88 us (2%)
    pallas_call x1, Pallas kernels, gather_blocks(): pl.pallas_call(functools.partial(gather_kernel, cut), out_shape=jax.Shape...  132 us
    pallas_call x1, Pallas kernels, teacher(): pl.pallas_call(functools.partial(teacher_kernel, feat_at, slots_w), out_s...  123 us
    pallas_call x1, Pallas kernels, reduce_grads(): pl.pallas_call(functools.partial(reduce_kernel, feat_coef, kl_coef, small...  80.3 us
    pallas_call x1, Pallas kernels, heads(): pl.pallas_call(functools.partial(heads_kernel, kl_coef, chunk), out_shape...  62.1 us
    pallas_call x1, Pallas kernels, place_blocks(): pl.pallas_call(functools.partial(place_kernel, n_head, lanes_u, lanes_p),...  40.9 us

profile of v2, /device:TPU:1, one launch (start us, length us, event | category | flops | bytes accessed | tf_op | source)
XLA Modules:
  0.0 447.4 jit_solution(14630538001413764773)
XLA Ops:
  0.6 0.0 copy-start.1
  0.6 0.9 copy-done.1
  1.6 0.0 copy-start.2
  1.6 0.9 copy-done.2
  2.5 0.0 copy-start.3
  2.5 0.9 copy-done.3
  3.4 0.0 copy-start.4
  3.4 0.7 copy-done.4
  4.1 122.9 %teacher.1 = (bf16[128,1024]{1,0:T(8,128)(2,1)S(1)}, bf16[128,1024]{1,0:T(8,128)(2,1)S(1)}, bf16[2,128,1024]{2,1,0:T(8,128)(2,1)S(1)}, bf16[4,2,128,384]{3,2,1,0:T(8,128)(2,1)}) custom-call(bf16[2,64,1024]{2,1,0:T(8,128)(2,1)S(1)} %copy-done.1, bf16[128,384]{1,0:T(8,128)(2,1)S(1)} %bitcast.11, f32[2,384]{1,0:T(2,128)S(1)} %copy-done.4, ...), custom_call_target="tpu_custom_call" | custom-call | flops 68719476736 | bytes 268435456 | tf_op jit(solution)/shard_map/teacher/pallas_call | solution.py:216
  127.0 0.0 copy-start
  127.0 0.8 copy-done
  127.8 0.0 copy-start.5
  127.8 0.7 copy-done.5
  128.5 0.0 copy-start.6
  128.5 0.7 copy-done.6
  129.2 62.1 %heads.1 = (f32[384,3840]{1,0:T(8,128)}, f32[128,384]{1,0:T(8,128)}, f32[8,128]{1,0:T(8,128)}) custom-call(bf16[2,128,1024]{2,1,0:T(8,128)(2,1)} %copy-done, bf16[1024,384]{1,0:T(8,128)(2,1)} %bitcast.14, bf16[15296,1024]{1,0:T(8,128)(2,1)} %bitcast.13, bf16[384,30592]{1,0:T(8,128)(2,1)} %hs_hbm.1), custom_call_target="tpu_custom_call" | custom-call | flops 4026531840 | bytes 3932160 | tf_op jit(solution)/shard_map/heads/pallas_call | solution.py:439
  191.3 80.3 %reduce.2.own_ref = f32[3,8,4992]{2,1,0:T(8,128)} custom-call(f32[4,4,24,3840]{3,2,1,0:T(8,128)} %bitcast.17, f32[128,384]{1,0:T(8,128)} %get-tuple-element.21.dx_ref, bf16[128,1024]{1,0:T(8,128)(2,1)} %copy-done.5, bf16[128,1024]{1,0:T(8,128)(2,1)} %copy-done.6, bf16[128,384]{1,0:T(8,128)(2,1)} %bitcast.10, f32[2,384]{1,0:T(2,128)} %gs_ref.3, ...), custom_call_target="tpu_custom_call" | custom-call | flops 1099511627776 | bytes 1474560 | tf_op jit(solution)/shard_map/reduce/pallas_call | solution.py:688
  271.6 132.3 %gather.1 = f32[2,4,4,4,3,8,4992]{6,5,4,3,2,1,0:T(8,128)} custom-call(f32[3,8,4992]{2,1,0:T(8,128)} %reduce.2.own_ref), custom_call_target="tpu_custom_call" | custom-call | flops 1099511627776 | bytes 61341696 | tf_op jit(solution)/shard_map/gather/pallas_call | solution.py:779
  403.9 40.9 %place.1 = (f32[16,3,8,30592]{3,2,1,0:T(8,128)}, f32[16,3,2,8,1536]{4,3,2,1,0:T(8,128)}, f32[4,16,3,2,8,384]{5,4,3,2,1,0:T(8,128)}, f32[2,16,3,8,1024]{4,3,2,1,0:T(8,128)}, f32[8,128]{1,0:T(8,128)}) custom-call(f32[2,4,16,3,8,4992]{5,4,3,2,1,0:T(8,128)} %bitcast.12), custom_call_target="tpu_custom_call" | custom-call | tf_op jit(solution)/shard_map/place/pallas_call | solution.py:880
  444.8 1.3 slice_reduce_fusion
  446.1 1.3 reshape.41
Async XLA Ops:
  0.6 1.0 copy-start.1
  1.6 0.9 copy-start.2
  2.5 0.9 copy-start.3
  3.4 0.7 copy-start.4
  127.0 0.8 copy-start
  127.8 0.7 copy-start.5
  128.5 0.7 copy-start.6

commit v3 on v2

--- a/solution.py
+++ b/solution.py
@@ -239,9 +239,9 @@
 
 def heads_kernel(kl_coef, chunk,
                  t_ref, r_ref, ht_hbm, hs_hbm,
-                 dw_hbm, dx_ref, kl_ref,
-                 tg, rt, ht, hs, zt, zs, mx, sm, st_send, st_all, lcol, grad, dx, px, ds, dr,
-                 ht_sem, hs_sem, ring_send, ring_recv, peer_send, peer_recv, st_send_sem, st_recv_sem, dx_send, dx_recv, out_sem):
+                 dw_hbm, dx, kl_ref,
+                 tg, rt, ht, hs, zt, zs, mx, sm, st_send, st_all, lcol, grad,
+                 ht_sem, hs_sem, ring_send, ring_recv, peer_send, peer_recv, st_send_sem, st_recv_sem, out_sem):
     coords = chip_coords()
     x = coords[X]
     core = lax.axis_index('tp')
@@ -332,15 +332,16 @@
         onward(k, opposite[k], way).start()
         across(opposite[k], core).start()
     lax.fori_loop(FAR, SIDE, student_logits, 0)
-    for k, way in enumerate(WAYS):
-        onward(k, FAR, way).wait_recv()
-    across(FAR, core).start()
     each_ht(lambda copy: copy.wait())
 
     def teacher_logits(i, _):
         for step, turn in ((RIGHT, 1), (LEFT, 2), (FAR, 3)):
             @pl.when(i == turn)
             def _():
+                if step == RIGHT:
+                    for k, way in enumerate(WAYS):
+                        onward(k, FAR, way).wait_recv()
+                    across(FAR, core).start()
                 across(step, 1 - core).wait_recv()
 
         b = at(jnp.where(i < FAR, i, SIDE + 1 - i))
@@ -405,20 +406,6 @@
     for copy in outs:
         copy.start()
 
-    for s in range(SIDE):
-        for c in CORES:
-            ds[c, s] = dx[lane_slice(2 * s + c, n_tok)]
-    swap = remote(ds.at[1 - core], px, dx_send.at[HERE], dx_recv.at[HERE], peer)
-    swap.start()
-    swap.wait()
-    ds[core] = ds[core] + px[...]
-    passes = [remote(ds.at[core, at(step)], dr.at[step - 1], dx_send.at[step], dx_recv.at[step], device(moved(coords, X, step), core))
-              for step in (RIGHT, FAR, LEFT)]
-    for copy in passes:
-        copy.start()
-    for copy in passes:
-        copy.wait()
-    dx_ref[...] = functools.reduce(jnp.add, [dr[i] for i in range(last_x)], ds[core, x])
     for k, way in enumerate(WAYS):
         first(k, HERE, way).wait_send()
         onward(k, opposite[k], way).wait_send()
@@ -438,7 +425,7 @@
     hops = (SIDE - 1,)
     return pl.pallas_call(
         functools.partial(heads_kernel, kl_coef, chunk),
-        out_shape=(jax.ShapeDtypeStruct((d_stud, cols), F32), jax.ShapeDtypeStruct((n_tok, d_stud), F32),
+        out_shape=(jax.ShapeDtypeStruct((d_stud, cols), F32), jax.ShapeDtypeStruct((n_all, d_stud), F32),
                    jax.ShapeDtypeStruct((SUBS, LANES), F32)),
         in_specs=[IN_VMEM, IN_VMEM, IN_HBM, IN_HBM],
         out_specs=(IN_HBM, IN_VMEM, IN_VMEM),
@@ -447,10 +434,8 @@
             v((SIDE, blk, cols), F32), v((SIDE, blk, cols), F32),
             v((len(PAIR), SIDE, blk, LANES), F32), v((len(PAIR), SIDE, blk, LANES), F32),
             v((SUBS, n_all), F32), v((n_peers + 1, SUBS, n_all), F32), v((n_all, LANES), F32),
-            v((n_all, chunk), BF16), v((n_all, d_stud), F32), v((SIDE, n_tok, d_stud), F32),
-            v((len(PAIR), SIDE, n_tok, d_stud), F32), v(hops + (n_tok, d_stud), F32),
-            DMA, DMA, DMA((SIDE,)), DMA((SIDE,)), DMA(hops), DMA(hops), DMA((n_peers,)), DMA((n_peers,)),
-            DMA((SIDE,)), DMA((SIDE,)), DMA((len(PAIR),)),
+            v((n_all, chunk), BF16),
+            DMA, DMA, DMA((SIDE,)), DMA((SIDE,)), DMA(hops), DMA(hops), DMA((n_peers,)), DMA((n_peers,)), DMA((len(PAIR),)),
         ],
         compiler_params=pltpu.CompilerParams(collective_id=collective_id, has_side_effects=True, vmem_limit_bytes=63 * MIB),
         cost_estimate=pl.CostEstimate(flops=d_model * n_all * cols, bytes_accessed=d_model * cols, transcendentals=0),
@@ -512,8 +497,8 @@
             src, dst = half.at[d, ..., pl.ds(0, n)], full.at[(d,) + lead + window]
         return remote(src, dst, send.at[i], recv.at[i], device(moved(self.coords, axis, way), self.core))
 
-    def start(self, k):
-        for turn in PAIR:
+    def start(self, k, turns=PAIR):
+        for turn in turns:
             for d in PAIR:
                 self.copy(k, turn, d).start()
 
@@ -556,7 +541,7 @@
 
 def reduce_kernel(feat_coef, kl_coef, small_parts,
                   dw, dx_ref, feat_a, feat_b, xs_ref, gs_ref, ups_ref, dns_ref, proj_ref, kl_ref,
-                  own, small, got, swap_send, swap_recv, *bufs):
+                  own, small, got, part_in, swap_send, swap_recv, in_send, in_recv, *bufs):
     coords = chip_coords()
     core = lax.axis_index('tp')
     peer = device(coords, 1 - core)
@@ -570,17 +555,22 @@
         return out
 
     head_jobs = [RingSum(coords, core, dw, (Y, Z), order, k * (cols // 2), take(2)) for k, order in enumerate(((Y, Z), (Z, Y)))]
+    in_job = RingSum(coords, core, part_in, (X,), (X,), 0, take(1))
     for job in head_jobs:
         job.start(0)
+    in_swap = remote(dx_ref.at[:, 1 - core], part_in, in_send, in_recv, peer)
+    in_swap.start()
 
     saved, _ = student_layers(xs_ref, gs_ref, ups_ref, dns_ref)
+    in_swap.wait()
+    part_in[...] = part_in[...] + dx_ref[:, core]
+    in_job.start(0)
     feats = (feat_a, feat_b)
     n_feat, d_in, d_mid = ups_ref.shape
     groups, yz, per_up, lanes_u, lanes_p, per_p, span = small_places(n_feat, d_in, d_mid, proj_ref.shape[-1])
     two = per_up // per_p
     err_rows = jnp.zeros((SUBS, LANES), F32)
-    resid_grad = None
-    gain_rows = []
+    out_grads, gain_rows = [], []
 
     def put(keep, chip_x, group, per, base, lanes, value):
         block, g = divmod(group, per)
@@ -588,9 +578,8 @@
         part, q = divmod(g, per // per_p)
         small[keep, chip_x, y, z, :, part * span + base + q * lanes:part * span + base + q * lanes + lanes] = value
 
-    for j in reversed(range(n_feat)):
-        unit, inv, normed, pre, act, unit_next, inv_next = saved[j]
-        proj_in = unit_next.astype(BF16)
+    for j in range(n_feat):
+        proj_in = saved[j][5].astype(BF16)
         err = dot(proj_in, proj_ref[j]) - feats[j][...].astype(F32)
         sq = err * err
         sq = functools.reduce(jnp.add, [sq[:, lane_slice(k, LANES)] for k in range(sq.shape[1] // LANES)])
@@ -600,11 +589,17 @@
         for i in range(groups):
             for cx in range(SIDE):
                 put(j, cx, i, per_p, two * lanes_u, lanes_p, g_proj[lane_slice(i, SUBS), lane_slice(cx, lanes_p)])
-        out_grad = dot_right_t(err_grad, proj_ref[j])
-        if resid_grad is None:
-            resid_grad = rms_back(unit_next, inv_next, out_grad + dx_ref[...])
-        else:
-            resid_grad = resid_grad + rms_back(unit_next, inv_next, out_grad)
+        out_grads.append(dot_right_t(err_grad, proj_ref[j]))
+    in_job.middle(0)
+    for job in head_jobs:
+        job.middle(0)
+    in_job.finish(0)
+    out_grads[-1] = out_grads[-1] + in_job.phases[-1][5][...]
+    resid_grad = None
+    for j in reversed(range(n_feat)):
+        unit, inv, normed, pre, act, unit_next, inv_next = saved[j]
+        step_grad = rms_back(unit_next, inv_next, out_grads[j])
+        resid_grad = step_grad if resid_grad is None else resid_grad + step_grad
         resid_bf = resid_grad.astype(BF16)
         g_down = dot_left_t(act, resid_bf)
         n_down = d_mid // SUBS
@@ -622,20 +617,26 @@
         if j > 0:
             resid_grad = resid_grad + rms_back(unit, inv, norm_grad * gs_ref[j:j + 1, :])
 
-    swaps = [remote(small.at[1 - core, cx], got.at[cx], swap_send.at[cx], swap_recv.at[cx], peer) for cx in range(SIDE)]
-    for copy in swaps:
-        copy.start()
-    for job in head_jobs:
-        job.middle(0)
-    for cx, copy in enumerate(swaps):
-        copy.wait()
-        got[cx] = got[cx] + small[core, cx]
+    def swap(step):
+        cx = lax.rem(coords[X] + step, SIDE)
+        return remote(small.at[1 - core, cx], got.at[cx], swap_send.at[step], swap_recv.at[step], peer)
+
+    order_in = (FAR, RIGHT, LEFT, HERE)
+    for step in order_in:
+        swap(step).start()
     lo = 0
     small_jobs = []
     for order, width in zip(ORDERS, small_parts):
         small_jobs.append(RingSum(coords, core, got, AXES, order, lo, take(3)))
         lo += width
-    for job in small_jobs:
+    first, rest = small_jobs[0], small_jobs[1:]
+    for step in order_in:
+        swap(step).wait()
+        cx = lax.rem(coords[X] + step, SIDE)
+        got[cx] = got[cx] + small[core, cx]
+        if step in (FAR, LEFT):
+            first.start(0, PAIR[step == LEFT:][:1])
+    for job in rest:
         job.start(0)
     for job in head_jobs:
         job.finish(0)
@@ -649,15 +650,13 @@
         job.start(1)
     for job in head_jobs:
         job.finish(1)
-    for job in small_jobs:
-        job.middle(1)
-    for job in small_jobs:
-        job.finish(1)
-        job.start(2)
-    for job in small_jobs:
-        job.middle(2)
-    for job in small_jobs:
-        job.finish(2)
+    for k in (1, 2):
+        for job in small_jobs:
+            job.middle(k)
+        for job in small_jobs:
+            job.finish(k)
+            if k < 2:
+                job.start(k + 1)
     for p in PARTS:
         for k, job in enumerate(head_jobs):
             own[p, :, lane_slice(k, cols // 2)] = job.phases[-1][5][lane_slice(p, SUBS), :]
@@ -670,19 +669,22 @@
         own[p, :, cols + span:] = jnp.zeros((SUBS, LANES), F32)
     for i, row in enumerate(gain_rows + [loss_row]):
         own[0, i:i + 1, cols + span:] = row
-    for job in head_jobs + small_jobs:
+    for job in head_jobs + small_jobs + [in_job]:
         job.drain()
 
 
 def reduce_grads(dw, dx, feats, x_stud, gain_s, w_up_s, w_down_s, proj_s, kl_tiles, feat_coef, kl_coef, collective_id,
-                 small_parts=(2048, 512, 512)):
+                 small_parts=(1280, 896, 896)):
     rows, cols = dw.shape[2:]
     span = sum(small_parts) // len(PARTS)
     width = cols // 2
+    xs_shape = x_stud.shape
     scratch = [pltpu.VMEM((len(PAIR), SIDE, SIDE, SIDE, SUBS, sum(small_parts)), F32),
-               pltpu.VMEM((SIDE, SIDE, SIDE, SUBS, sum(small_parts)), F32), DMA((SIDE,)), DMA((SIDE,))]
+               pltpu.VMEM((SIDE, SIDE, SIDE, SUBS, sum(small_parts)), F32), pltpu.VMEM((SIDE,) + xs_shape, F32),
+               DMA((SIDE,)), DMA((SIDE,)), DMA, DMA]
     for _ in PAIR:
         scratch += RingSum.shapes((Y, Z), (Y, Z), rows, width)
+    scratch += RingSum.shapes((X,), (X,), *xs_shape)
     for part in small_parts:
         scratch += RingSum.shapes(AXES, AXES, SUBS, part)
     return pl.pallas_call(
@@ -698,6 +700,9 @@
 
 
 ALL = pl.ds(0, SIDE)
+WHOLE, LOW, HIGH = range(SIDE - 1)
+SOURCE = (LEFT, RIGHT)
+ARRIVAL = (HERE, LEFT, RIGHT, FAR)
 
 
 def gather_kernel(cut, own_ref, full, own_sem, send_sem, recv_sem, peer_send, peer_recv):
@@ -710,185 +715,161 @@
     for copy in here:
         copy.start()
     greet(near_targets(coords, core))
-    whole, low, high = range(3)
 
     def lanes(part, span):
-        return pl.ds(cut if span == high else 0, (widths[part], cut, widths[part] - cut)[span])
-
-    def at_of(part, phase, step):
-        return lax.rem(coords[ORDERS[part][phase]] + step, SIDE)
-
-    def block(part, phase, step, span):
+        return pl.ds(cut if span == HIGH else 0, (widths[part], cut, widths[part] - cut)[span])
+
+    def block(part, steps, span=WHOLE):
         idx = list(coords)
-        for k, axis in enumerate(ORDERS[part][:phase + 1]):
-            idx[axis] = ALL if k < phase else at_of(part, phase, step)
+        for axis, step in zip(ORDERS[part], steps):
+            idx[axis] = ALL if step is ALL else lax.rem(coords[axis] + step, SIDE)
         return full.at[(core,) + tuple(idx) + (part, slice(None), lanes(part, span))]
 
-    def ring(part, phase, slot, step, span):
-        dst = block(part, phase, step, span)
-        src = own_ref.at[part, :, lanes(part, span)] if phase == 0 and step == HERE else dst
-        return remote(src, dst, send_sem.at[part, phase, slot], recv_sem.at[part, phase, slot],
-                      device(moved(coords, ORDERS[part][phase], WAYS[slot % 2]), core))
-
-    def first(part, phase, d, step):
-        return ring(part, phase, d, step, whole)
-
-    def onward(part, phase, d, step):
-        return ring(part, phase, d + 2, step, (low, high)[d])
-
-    def across(part, phase, step):
-        src = block(part, phase, step, whole)
-        return remote(src, src, peer_send.at[part, phase, step], peer_recv.at[part, phase, step], peer)
-
-    def own_across(part):
-        dst = block(part, 0, HERE, whole)
-        return remote(own_ref.at[part, :, lanes(part, whole)], dst, peer_send.at[part, 0, HERE], peer_recv.at[part, 0, HERE], peer)
-
-    source = (LEFT, RIGHT)
+    def steps_of(phase, sub, step):
+        return ((step,), (sub, step), (ALL, sub, step))[phase]
+
+    def ring(part, phase, sub, slot, step, span):
+        dst = block(part, steps_of(phase, sub, step), span)
+        mine = step == HERE and (phase == 0 or (phase == 1 and sub == HERE))
+        src = own_ref.at[part, :, lanes(part, span)] if mine else dst
+        at = (part, phase, sub, slot)
+        return remote(src, dst, send_sem.at[at], recv_sem.at[at], device(moved(coords, ORDERS[part][phase], WAYS[slot % 2]), core))
+
+    def first(part, phase, sub, d, step):
+        return ring(part, phase, sub, d, step, WHOLE)
+
+    def onward(part, phase, sub, d, step):
+        return ring(part, phase, sub, d + 2, step, (LOW, HIGH)[d])
+
+    def send(part, phase, sub):
+        for d in PAIR:
+            first(part, phase, sub, d, HERE).start()
+
+    def relay(part, phase, sub, d):
+        first(part, phase, sub, d, SOURCE[d]).wait_recv()
+        onward(part, phase, sub, d, SOURCE[d]).start()
+
+    def far_in(part, phase, sub):
+        for d in PAIR:
+            onward(part, phase, sub, d, FAR).wait_recv()
+
+    def across(part, phase, sub, step):
+        dst = block(part, ((step,), (ALL, step), (ALL, sub, step))[phase])
+        src = own_ref.at[part, :, lanes(part, WHOLE)] if phase == 0 and step == HERE else dst
+        at = (part, phase, sub, step)
+        return remote(src, dst, peer_send.at[at], peer_recv.at[at], peer)
+
+    for part in PARTS:
+        send(part, 0, HERE)
+    for part in PARTS:
+        send(part, 1, HERE)
+        across(part, 0, HERE, HERE).start()
     for part in PARTS:
         for d in PAIR:
-            first(part, 0, d, HERE).start()
-        own_across(part).start()
-    for phase in AXES:
+            relay(part, 0, HERE, d)
+            send(part, 1, SOURCE[d])
+            across(part, 0, HERE, SOURCE[d]).start()
+    for part in PARTS:
+        far_in(part, 0, HERE)
+        send(part, 1, FAR)
+        across(part, 0, HERE, FAR).start()
+        here[part].wait()
+        send(part, 2, HERE)
+    for sub in ARRIVAL:
         for part in PARTS:
             for d in PAIR:
-                first(part, phase, d, source[d]).wait_recv()
-                onward(part, phase, d, source[d]).start()
-                across(part, phase, source[d]).start()
+                relay(part, 1, sub, d)
+                if sub == FAR:
+                    send(part, 2, SOURCE[d])
+                    across(part, 1, HERE, SOURCE[d]).start()
+    for part in PARTS:
+        for sub in ARRIVAL:
+            far_in(part, 1, sub)
+        send(part, 2, FAR)
+        across(part, 1, HERE, FAR).start()
+    for sub in ARRIVAL:
         for part in PARTS:
             for d in PAIR:
-                onward(part, phase, d, FAR).wait_recv()
-            if phase == 0:
-                here[part].wait()
-            if phase < AXES[-1]:
-                for d in PAIR:
-                    first(part, phase + 1, d, HERE).start()
-            across(part, phase, FAR).start()
+                relay(part, 2, sub, d)
+                across(part, 2, sub, SOURCE[d]).start()
+    for sub in ARRIVAL:
+        for part in PARTS:
+            far_in(part, 2, sub)
+            across(part, 2, sub, FAR).start()
     for part in PARTS:
         for phase in AXES:
-            for d in PAIR:
-                first(part, phase, d, HERE).wait_send()
-                onward(part, phase, d, source[d]).wait_send()
-            for step in (LEFT, RIGHT, FAR):
-                across(part, phase, step).wait()
-        own_across(part).wait()
+            for sub in ARRIVAL if phase else (HERE,):
+                for d in PAIR:
+                    first(part, phase, sub, d, HERE).wait_send()
+                    onward(part, phase, sub, d, SOURCE[d]).wait_send()
+                for step in ARRIVAL if phase == 0 else (LEFT, RIGHT, FAR):
+                    if phase != 1 or sub == HERE:
+                        across(part, phase, sub, step).wait()
 
 
 def gather_blocks(own, cut, collective_id):
-    sems = DMA((len(PARTS), len(AXES), SIDE))
+    sems = DMA((len(PARTS), len(AXES), SIDE, SIDE))
     return pl.pallas_call(
         functools.partial(gather_kernel, cut),
-        out_shape=jax.ShapeDtypeStruct((len(PAIR), SIDE, SIDE, SIDE) + own.shape, F32),
+        out_shape=pltpu.VMEM((len(PAIR), SIDE, SIDE, SIDE) + own.shape, F32),
         in_specs=[IN_VMEM],
         out_specs=IN_HBM,
         scratch_shapes=[DMA((len(PARTS),)), sems, sems, sems, sems],
-        compiler_params=pltpu.CompilerParams(collective_id=collective_id, has_side_effects=True),
+        compiler_params=pltpu.CompilerParams(collective_id=collective_id, has_side_effects=True, vmem_limit_bytes=MIB),
         cost_estimate=pl.CostEstimate(flops=MIB * MIB, bytes_accessed=SIDE * LANES * own.size, transcendentals=0),
         name='gather',
     )(own)
 
 
-N_BUF = 6
-N_LATE = N_BUF // 2
-
-
 def place_kernel(n_head, lanes_u, lanes_p,
                  full, head, up, down, proj, total,
-                 bufs, edge, wide, narrow, tiles,
-                 in_sem, out_sem, edge_sem, wide_in, wide_out, narrow_in, narrow_out, tile_sem):
+                 edge, head_sem, edge_sem, wide_sem, narrow_sem):
     last_x = SIDE - 1
-    per = wide.shape[3]
+    per = up.shape[3]
     copy = pltpu.make_async_copy
     narrow_at = n_head + per * lanes_u
-    tile_copy = copy(full.at[:, :, :, 0, :, pl.ds(narrow_at + lanes_p, LANES)], tiles, tile_sem)
-    tile_copy.start()
-    owners = [(c, x) for c in CORES for x in range(SIDE)]
-    jobs = [owner + (s,) for owner in owners for s in range(SIDE)]
-
-    def fetch(i):
-        c, x, s = jobs[i]
-        slot = i % N_BUF
-        blocks = pl.ds(s * SIDE, SIDE)
-        out = [copy(full.at[c, x, blocks, :, :, pl.ds(0, n_head)], bufs.at[slot], in_sem.at[slot])]
-        if (c, x) == PAIR[::-1]:
-            out.append(copy(full.at[0, last_x, blocks, :, :, pl.ds(n_head - LANES, LANES)], edge.at[slot], edge_sem.at[slot]))
-        return out
-
-    def put(i):
-        c, x, s = jobs[i]
-        slot = i % N_BUF
-        n = n_head - LANES if (c, x) == (0, last_x) else n_head
-        at = (c * SIDE + x) * n_head - c * LANES
-        return copy(bufs.at[slot, :, :, :, pl.ds(0, n)], head.at[pl.ds(s * SIDE, SIDE), :, :, pl.ds(at, n)], out_sem.at[slot])
-
-    def small_fetch(i):
-        c, x = owners[i]
-        slot = i % 2
-        out = [copy(full.at[c, x, :, :, :, pl.ds(n_head + q * lanes_u, lanes_u)], wide.at[slot, :, :, q], wide_in.at[slot, q])
-               for q in range(per)]
-        return out + [copy(full.at[c, x, :, :, :, pl.ds(narrow_at, lanes_p)], narrow.at[slot], narrow_in.at[slot])]
-
-    def small_put(i):
-        c, x = owners[i]
-        slot = i % 2
-        dst = down.at[x] if c else up.at[:, :, :, :, pl.ds(x * lanes_u, lanes_u)]
-        return [copy(wide.at[slot], dst, wide_out.at[slot]),
-                copy(narrow.at[slot], proj.at[c, :, :, :, pl.ds(x * lanes_p, lanes_p)], narrow_out.at[slot])]
-
-    def each(copies, act):
-        for one in copies:
-            act(one)
-
-    start, wait = (lambda one: one.start()), (lambda one: one.wait())
-    for i in range(N_LATE):
-        each(fetch(i), start)
-    each(small_fetch(0), start)
-    for i in range(len(jobs)):
-        nxt = i + N_LATE
-        if nxt < len(jobs):
-            if nxt >= N_BUF:
-                wait(put(nxt - N_BUF))
-            each(fetch(nxt), start)
-        each(fetch(i), wait)
-        if jobs[i][:2] == PAIR[::-1]:
-            slot = i % N_BUF
-            bufs[slot, :, :, :, :LANES] = bufs[slot, :, :, :, :LANES] + edge[slot]
-        start(put(i))
-        if i % SIDE == SIDE - 1:
-            k = i // SIDE
-            each(small_fetch(k), wait)
-            each(small_put(k), start)
-            if k:
-                each(small_put(k - 1), wait)
-            if k + 1 < len(owners):
-                each(small_fetch(k + 1), start)
-    tile_copy.wait()
-    sums = jnp.sum(tiles[...].reshape(-1, SUBS, LANES), axis=0)
-    total[...] = sums
-    for i in range(len(jobs) - N_BUF, len(jobs)):
-        wait(put(i))
-    each(small_put(len(owners) - 1), wait)
+    copies = []
+    for c in CORES:
+        for x in range(SIDE):
+            src = full.at[c, x]
+            lo = LANES if (c, x) == PAIR[::-1] else 0
+            hi = n_head - LANES if (c, x) == (0, last_x) else n_head
+            at = (c * SIDE + x) * n_head - c * LANES
+            copies.append(copy(src.at[:, :, :, :, pl.ds(lo, hi - lo)], head.at[:, :, :, :, pl.ds(at + lo, hi - lo)], head_sem.at[c, x]))
+            for q in range(per):
+                dst = down.at[x, :, :, :, q] if c else up.at[:, :, :, q, :, pl.ds(x * lanes_u, lanes_u)]
+                copies.append(copy(src.at[:, :, :, :, pl.ds(n_head + q * lanes_u, lanes_u)], dst, wide_sem.at[c, x, q]))
+            copies.append(copy(src.at[:, :, :, :, pl.ds(narrow_at, lanes_p)], proj.at[c, :, :, :, :, pl.ds(x * lanes_p, lanes_p)],
+                               narrow_sem.at[c, x]))
+    for one in copies:
+        one.start()
+    edge[...] = full[0, last_x, :, :, :, :, n_head - LANES:n_head] + full[1, 0, :, :, :, :, :LANES]
+    edge_copy = copy(edge, head.at[:, :, :, :, pl.ds(SIDE * n_head - LANES, LANES)], edge_sem)
+    edge_copy.start()
+    tiles = full[:, :, :, :, 0, :, narrow_at + lanes_p:narrow_at + lanes_p + LANES]
+    total[...] = jnp.sum(tiles.reshape(-1, SUBS, LANES), axis=0)
+    edge_copy.wait()
+    for one in copies:
+        one.wait()
 
 
 def place_blocks(full, n_head, lanes_u, lanes_p, vocab):
-    _, _, n_yz, n_part, subs, _ = full.shape
+    n_part, subs, _ = full.shape[4:]
     per = len(PAIR)
-    v = pltpu.VMEM
     pair = (len(PAIR),)
-    shapes = ((n_yz, n_part, subs, vocab), (n_yz, n_part, per, subs, SIDE * lanes_u), (SIDE, n_yz, n_part, per, subs, lanes_u),
-              pair + (n_yz, n_part, subs, SIDE * lanes_p), (subs, LANES))
+    owners = pair + (SIDE,)
+    yz = (SIDE, SIDE)
+    shapes = (yz + (n_part, subs, vocab), yz + (n_part, per, subs, SIDE * lanes_u), (SIDE,) + yz + (n_part, per, subs, lanes_u),
+              pair + yz + (n_part, subs, SIDE * lanes_p), (subs, LANES))
     return pl.pallas_call(
         functools.partial(place_kernel, n_head, lanes_u, lanes_p),
         out_shape=tuple(jax.ShapeDtypeStruct(s, F32) for s in shapes),
-        in_specs=[IN_HBM],
+        in_specs=[IN_VMEM],
         out_specs=(IN_HBM,) * SIDE + (IN_VMEM,),
-        scratch_shapes=[v((N_BUF, SIDE, n_part, subs, n_head), F32), v((N_BUF, SIDE, n_part, subs, LANES), F32),
-                        v(pair + (n_yz, n_part, per, subs, lanes_u), F32), v(pair + (n_yz, n_part, subs, lanes_p), F32),
-                        v(pair + (SIDE, n_yz, subs, LANES), F32),
-                        DMA((N_BUF,)), DMA((N_BUF,)), DMA((N_BUF,)), DMA(pair + (per,)), DMA(pair), DMA(pair), DMA(pair), DMA],
-        compiler_params=pltpu.CompilerParams(has_side_effects=True, vmem_limit_bytes=56 * MIB),
+        scratch_shapes=[pltpu.VMEM(yz + (n_part, subs, LANES), F32), DMA(owners), DMA, DMA(owners + (per,)), DMA(owners)],
+        compiler_params=pltpu.CompilerParams(has_side_effects=True, vmem_limit_bytes=MIB),
         name='place',
-    )(full)
+    )(pltpu.with_memory_space_constraint(full, pltpu.VMEM))
 
 
 def solution(mesh):
@@ -903,12 +884,11 @@
         xs = x_stud[0]
         feat_one, feat_two, states, stud_all = teacher(x_teach, xs, gain_s, w_up_s, w_down_s, gain_t, w_up_t, w_down_t,
                                                        w_up_t.shape[0] // n_feat, 0)
-        head_part, head_in_grad, kl_tiles = heads(states, stud_all.reshape(-1, d_in), head_t, head_s, kl_coef, 1)
+        head_part, in_part, kl_tiles = heads(states, stud_all.reshape(-1, d_in), head_t, head_s, kl_coef, 1)
         cols = head_part.shape[1]
-        own = reduce_grads(head_part.reshape(SIDE, SIDE, -1, cols), head_in_grad, (feat_one, feat_two), xs, gain_s, w_up_s, w_down_s,
+        own = reduce_grads(head_part.reshape(SIDE, SIDE, -1, cols), in_part.reshape((SIDE, -1) + xs.shape), (feat_one, feat_two), xs, gain_s, w_up_s, w_down_s,
                            proj_s, kl_tiles, feat_coef, kl_coef, 2)
         blocks = gather_blocks(own, 20 * LANES, 3)
-        blocks = blocks.reshape(blocks.shape[:2] + (SIDE * SIDE,) + blocks.shape[-3:])
         head_grad, up, down, proj, total = place_blocks(blocks, cols, d_mid // SIDE, d_teach // SIDE, head_s.shape[1])
         n_gain = n_feat * d_in // LANES
         return (jnp.sum(total[n_gain]), up.reshape(w_up_s.shape), down.reshape(w_down_s.shape), total[:n_gain].reshape(gain_s.shape),

time: 448 us -> 399 us (0.89)
  Pallas kernels: 439 us -> 390 us
    pallas_call x1, Pallas kernels: 40.9 us -> 19.7 us  [place_blocks(): pl.pallas_call(functools.partial(place_kernel, n_head, lanes_u, lanes_p),...]
    pallas_call x1, Pallas kernels: 62.1 us -> 50.1 us  [heads(): pl.pallas_call(functools.partial(heads_kernel, kl_coef, chunk), out_shape...]
    pallas_call x1, Pallas kernels: 80.3 us -> 71.9 us  [reduce_grads(): pl.pallas_call(functools.partial(reduce_kernel, feat_coef, kl_coef, small...]
    pallas_call x1, Pallas kernels: 132 us -> 125 us  [gather_blocks(): pl.pallas_call(functools.partial(gather_kernel, cut), out_shape=pltpu.VME...]
where the time goes in v3:
time: 399 us; the launch traced here: 398 us
  Pallas kernels  390 us (98%)
  local copies, waits for them, and re-layouts  6.87 us (2%)
    pallas_call x1, Pallas kernels, gather_blocks(): pl.pallas_call(functools.partial(gather_kernel, cut), out_shape=pltpu.VME...  125 us
    pallas_call x1, Pallas kernels, teacher(): pl.pallas_call(functools.partial(teacher_kernel, feat_at, slots_w), out_s...  123 us
    pallas_call x1, Pallas kernels, reduce_grads(): pl.pallas_call(functools.partial(reduce_kernel, feat_coef, kl_coef, small...  71.9 us
    pallas_call x1, Pallas kernels, heads(): pl.pallas_call(functools.partial(heads_kernel, kl_coef, chunk), out_shape...  50.1 us
    pallas_call x1, Pallas kernels, place_blocks(): pl.pallas_call(functools.partial(place_kernel, n_head, lanes_u, lanes_p),...  19.7 us

profile of v3, /device:TPU:1, one launch (start us, length us, event | category | flops | bytes accessed | tf_op | source)
XLA Modules:
  0.0 398.4 jit_solution(7022840164470794078)
XLA Ops:
  0.6 0.0 copy-start.1
  0.6 0.9 copy-done.1
  1.6 0.0 copy-start.2
  1.6 0.9 copy-done.2
  2.5 0.0 copy-start.3
  2.5 0.9 copy-done.3
  3.4 0.0 copy-start.4
  3.4 0.7 copy-done.4
  4.1 122.9 %teacher.1 = (bf16[128,1024]{1,0:T(8,128)(2,1)S(1)}, bf16[128,1024]{1,0:T(8,128)(2,1)S(1)}, bf16[2,128,1024]{2,1,0:T(8,128)(2,1)S(1)}, bf16[4,2,128,384]{3,2,1,0:T(8,128)(2,1)}) custom-call(bf16[2,64,1024]{2,1,0:T(8,128)(2,1)S(1)} %copy-done.1, bf16[128,384]{1,0:T(8,128)(2,1)S(1)} %bitcast.11, f32[2,384]{1,0:T(2,128)S(1)} %copy-done.4, ...), custom_call_target="tpu_custom_call" | custom-call | flops 68719476736 | bytes 268435456 | tf_op jit(solution)/shard_map/teacher/pallas_call | solution.py:216
  127.0 0.0 copy-start
  127.0 0.8 copy-done
  127.8 0.0 copy-start.5
  127.8 0.7 copy-done.5
  128.5 0.0 copy-start.6
  128.5 0.7 copy-done.6
  129.2 50.1 %heads.1 = (f32[384,3840]{1,0:T(8,128)}, f32[1024,384]{1,0:T(8,128)}, f32[8,128]{1,0:T(8,128)}) custom-call(bf16[2,128,1024]{2,1,0:T(8,128)(2,1)} %copy-done, bf16[1024,384]{1,0:T(8,128)(2,1)} %bitcast.13, bf16[15296,1024]{1,0:T(8,128)(2,1)} %bitcast.12, bf16[384,30592]{1,0:T(8,128)(2,1)} %hs_hbm.1), custom_call_target="tpu_custom_call" | custom-call | flops 4026531840 | bytes 3932160 | tf_op jit(solution)/shard_map/heads/pallas_call | solution.py:426
  179.2 71.9 %reduce.2.own_ref = f32[3,8,4992]{2,1,0:T(8,128)} custom-call(f32[4,4,24,3840]{3,2,1,0:T(8,128)} %bitcast.16, f32[4,2,128,384]{3,2,1,0:T(8,128)} %bitcast.20, bf16[128,1024]{1,0:T(8,128)(2,1)} %copy-done.5, bf16[128,1024]{1,0:T(8,128)(2,1)} %copy-done.6, bf16[128,384]{1,0:T(8,128)(2,1)} %bitcast.10, f32[2,384]{1,0:T(2,128)} %gs_ref.3, ...), custom_call_target="tpu_custom_call" | custom-call | flops 1099511627776 | bytes 1474560 | tf_op jit(solution)/shard_map/reduce/pallas_call | solution.py:690
  251.2 125.0 %gather.1.full = f32[2,4,4,4,3,8,4992]{6,5,4,3,2,1,0:T(8,128)S(1)} custom-call(f32[3,8,4992]{2,1,0:T(8,128)} %reduce.2.own_ref), custom_call_target="tpu_custom_call" | custom-call | flops 1099511627776 | bytes 61341696 | tf_op jit(solution)/shard_map/gather/pallas_call | solution.py:812
  376.1 19.7 %place.1 = (f32[4,4,3,8,30592]{4,3,2,1,0:T(8,128)}, f32[4,4,3,2,8,1536]{5,4,3,2,1,0:T(8,128)}, f32[4,4,4,3,2,8,384]{6,5,4,3,2,1,0:T(8,128)}, f32[2,4,4,3,8,1024]{5,4,3,2,1,0:T(8,128)}, f32[8,128]{1,0:T(8,128)}) custom-call(f32[2,4,4,4,3,8,4992]{6,5,4,3,2,1,0:T(8,128)S(1)} %gather.1.full), custom_call_target="tpu_custom_call" | custom-call | tf_op jit(solution)/shard_map/place/pallas_call | solution.py:864
  395.9 1.3 slice_reduce_fusion
  397.2 1.3 reshape.41
Async XLA Ops:
  0.6 1.0 copy-start.1
  1.6 0.9 copy-start.2
  2.5 0.9 copy-start.3
  3.4 0.7 copy-start.4
  127.0 0.8 copy-start
  127.8 0.7 copy-start.5
  128.5 0.7 copy-start.6

commit v4 on v3

--- a/solution.py
+++ b/solution.py
@@ -83,6 +83,10 @@
     return half + half * jnp.tanh(u * (GELU_C + (GELU_C * GELU_K) * (u * u)))
 
 
+def gelu_of_half(v):
+    return v + v * jnp.tanh(v * (2 * GELU_C + (8 * GELU_C * GELU_K) * (v * v)))
+
+
 def gelu_slope(u):
     sq = u * u
     t = jnp.tanh(u * (GELU_C + (GELU_C * GELU_K) * sq))
@@ -117,15 +121,16 @@
 
 
 def teacher_kernel(feat_at, slots_w,
-                   x_ref, xs_ref, gs_ref, ups_ref, dns_ref, gain_ref, wup_hbm, wdn_hbm,
-                   feat_ref, last_ref, state_ref, group_ref,
-                   h, nrm, act, wu, wd, part, got, r_own,
-                   usem, dsem, xsend, xrecv, ssem, rsem, gsend, grecv):
+                   x_hbm, xs_hbm, gs_hbm, ups_hbm, dns_hbm, gain_hbm, wup_hbm, wdn_hbm,
+                   feat_hbm, last_hbm, state_hbm, group_hbm,
+                   xs_ref, gs_ref, ups_ref, dns_ref, gain_ref, feat_ref, last_ref, state_ref, h, nrm, wu, wd, part, got, r_own,
+                   in_sems, out_sems, usem, dsem, xown, xsend, xrecv, ssem, rsem, gsend, grecv):
     me = lax.axis_index('tp')
     coords = chip_coords()
     peer = device(coords, 1 - me)
     n_layers = gain_ref.shape[0]
-    rows, seq_half, d_model = x_ref.shape
+    rows, seq_half, d_model = x_hbm.shape
+    d_ff = wu.shape[-1]
 
     def up_copy(layer, slot):
         return pltpu.make_async_copy(wup_hbm.at[layer], wu.at[slot], usem.at[slot])
@@ -133,23 +138,31 @@
     def down_copy(layer, slot):
         return pltpu.make_async_copy(wdn_hbm.at[layer], wd.at[slot], dsem.at[slot])
 
+    ins = [pltpu.make_async_copy(src, dst, in_sems.at[i]) for i, (src, dst) in enumerate((
+        (xs_hbm, xs_ref), (gs_hbm, gs_ref), (ups_hbm, ups_ref), (dns_hbm, dns_ref), (gain_hbm, gain_ref)))]
+    mine = pl.ds(pl.multiple_of(me * seq_half, seq_half), seq_half)
+    xcopy_own = pltpu.make_async_copy(x_hbm, h.at[:, mine], xown)
+    for copy in ins + [xcopy_own]:
+        copy.start()
     for i in range(slots_w):
         up_copy(i, i).start()
         down_copy(i, i).start()
     targets = group_targets(coords, me)
     greet(targets)
-    mine = pl.ds(pl.multiple_of(me * seq_half, seq_half), seq_half)
-    xcopy = remote(x_ref, h.at[:, mine], xsend, xrecv, peer)
+    xcopy = remote(x_hbm, h.at[:, mine], xsend, xrecv, peer)
     xcopy.start()
-    h[:, mine] = x_ref[...]
+    for copy in ins:
+        copy.wait()
 
     _, head_in = student_layers(xs_ref, gs_ref, ups_ref, dns_ref)
     r_own[...] = head_in
-    r_copies = [remote(r_own, group_ref.at[coords[X], me], gsend.at[i], grecv.at[i], target) for i, target in enumerate(targets)]
+    r_copies = [remote(r_own, group_hbm.at[coords[X], me], gsend.at[i], grecv.at[i], target) for i, target in enumerate(targets)]
     for copy in r_copies:
         copy.start()
-    group_ref[coords[X], me] = head_in
+    r_keep = pltpu.make_async_copy(r_own, group_hbm.at[coords[X], me], out_sems.at[SIDE - 1])
+    r_keep.start()
     xcopy.wait()
+    xcopy_own.wait()
 
     def p_copy(ck, slot):
         return remote(part.at[ck, slot], got.at[ck, slot], ssem.at[ck, slot], rsem.at[ck, slot], peer)
@@ -157,7 +170,7 @@
     def update(ck, slot):
         p_copy(ck, slot).wait()
         total = part[ck, slot] + got[ck, slot]
-        h[ck] = (h[ck].astype(F32) + total.astype(BF16).astype(F32)).astype(BF16)
+        h[ck] = h[ck] + total.astype(BF16)
 
     def layer_step(layer, _):
         slot = lax.rem(layer, len(PAIR))
@@ -174,21 +187,20 @@
                 feat_ref[...] = h[ck]
 
             unit, _ = rms_unit(h[ck].astype(F32))
-            nrm[...] = (unit * gain_ref[pl.ds(layer, 1), :]).astype(BF16)
+            nrm[...] = (unit * (0.5 * gain_ref[pl.ds(layer, 1), :])).astype(BF16)
             if first:
                 up_copy(layer, ws).wait()
-            act[...] = gelu_act(dot(nrm[...], wu[ws])).astype(BF16)
+                down_copy(layer, ws).wait()
+            halves = []
+            for piece in (slice(None, d_ff // 2), slice(d_ff // 2, None)):
+                act = gelu_of_half(dot(nrm[...], wu[ws, :, piece])).astype(BF16)
+                halves.append(dot(act, wd[ws, piece, :]))
+            part[ck, slot] = halves[0] + halves[1]
+            p_copy(ck, slot).start()
             if last:
                 @pl.when(layer + slots_w < n_layers)
                 def _():
                     up_copy(layer + slots_w, ws).start()
-            if first:
-                down_copy(layer, ws).wait()
-            part[ck, slot] = dot(act[...], wd[ws])
-            p_copy(ck, slot).start()
-            if last:
-                @pl.when(layer + slots_w < n_layers)
-                def _():
                     down_copy(layer + slots_w, ws).start()
         return 0
 
@@ -201,7 +213,11 @@
             last_ref[...] = h[ck]
 
         state_ref[ck] = rms_unit(h[ck].astype(F32))[0].astype(BF16)
-    for copy in r_copies:
+    outs = [pltpu.make_async_copy(src, dst, out_sems.at[i])
+            for i, (src, dst) in enumerate(((feat_ref, feat_hbm), (last_ref, last_hbm), (state_ref, state_hbm)))]
+    for copy in outs:
+        copy.start()
+    for copy in r_copies + outs + [r_keep]:
         copy.wait()
 
 
@@ -213,23 +229,25 @@
     feat = jax.ShapeDtypeStruct((n_tok, d_model), BF16)
     slots = (rows, len(PAIR))
     weights = n_layers * d_model * d_ff
+    args = (x_teach, x_stud, gain_s, w_up_s, w_down_s, gain_t, w_up_t, w_down_t)
     return pl.pallas_call(
         functools.partial(teacher_kernel, feat_at, slots_w),
         out_shape=(feat, feat, jax.ShapeDtypeStruct((rows, n_tok, d_model), BF16),
                    jax.ShapeDtypeStruct((SIDE, len(PAIR)) + x_stud.shape, BF16)),
-        in_specs=[IN_VMEM] * 6 + [IN_HBM] * len(PAIR),
-        out_specs=(IN_VMEM,) * SIDE,
-        scratch_shapes=[
-            pltpu.VMEM((rows, n_tok, d_model), BF16), pltpu.VMEM((n_tok, d_model), BF16), pltpu.VMEM((n_tok, d_ff), BF16),
+        in_specs=[IN_HBM] * len(args),
+        out_specs=(IN_HBM,) * SIDE,
+        scratch_shapes=[pltpu.VMEM(a.shape, a.dtype) for a in args[1:-len(PAIR)]] + [
+            pltpu.VMEM((n_tok, d_model), BF16), pltpu.VMEM((n_tok, d_model), BF16), pltpu.VMEM((rows, n_tok, d_model), BF16),
+            pltpu.VMEM((rows, n_tok, d_model), BF16), pltpu.VMEM((n_tok, d_model), BF16),
             pltpu.VMEM((slots_w, d_model, d_ff), BF16), pltpu.VMEM((slots_w, d_ff, d_model), BF16),
             pltpu.VMEM(slots + (n_tok, d_model), F32), pltpu.VMEM(slots + (n_tok, d_model), F32),
             pltpu.VMEM(x_stud.shape, BF16),
-            DMA((slots_w,)), DMA((slots_w,)), DMA, DMA, DMA(slots), DMA(slots), DMA((n_peers,)), DMA((n_peers,)),
+            DMA((len(args),)), DMA((SIDE,)), DMA((slots_w,)), DMA((slots_w,)), DMA, DMA, DMA, DMA(slots), DMA(slots), DMA((n_peers,)), DMA((n_peers,)),
         ],
-        compiler_params=pltpu.CompilerParams(collective_id=collective_id, has_side_effects=True, vmem_limit_bytes=52 * MIB),
+        compiler_params=pltpu.CompilerParams(collective_id=collective_id, has_side_effects=True, vmem_limit_bytes=63 * MIB),
         cost_estimate=pl.CostEstimate(flops=SIDE * rows * n_tok * weights, bytes_accessed=SIDE * weights, transcendentals=0),
         name='teacher',
-    )(x_teach, x_stud, gain_s, w_up_s, w_down_s, gain_t, w_up_t, w_down_t)
+    )(*args)
 
 
 NEG = -1e38
@@ -238,15 +256,15 @@
 
 
 def heads_kernel(kl_coef, chunk,
-                 t_ref, r_ref, ht_hbm, hs_hbm,
+                 t_hbm, r_hbm, ht_hbm, hs_hbm,
                  dw_hbm, dx, kl_ref,
-                 tg, rt, ht, hs, zt, zs, mx, sm, st_send, st_all, lcol, grad,
-                 ht_sem, hs_sem, ring_send, ring_recv, peer_send, peer_recv, st_send_sem, st_recv_sem, out_sem):
+                 r_ref, tg, rt, ht, hs, zt, zs, mx, sm, st_send, st_all, lcol, grad,
+                 ht_sem, hs_sem, t_sem, r_sem, ring_send, ring_recv, peer_send, peer_recv, st_send_sem, st_recv_sem, out_sem):
     coords = chip_coords()
     x = coords[X]
     core = lax.axis_index('tp')
     peer = device(coords, 1 - core)
-    rows, n_tok, d_model = t_ref.shape
+    rows, n_tok, d_model = t_hbm.shape
     d_stud, cols = hs.shape
     n_tiles = cols // LANES
     blk = rows * n_tok
@@ -257,6 +275,10 @@
     first_tile = n_tiles * x + core * (n_tiles * SIDE - 1)
     hs_copy = pltpu.make_async_copy(hs_hbm.at[:, pl.ds(pl.multiple_of(first_tile * LANES, LANES), cols)], hs, hs_sem)
     hs_copy.start()
+    r_copy = pltpu.make_async_copy(r_hbm, r_ref, r_sem)
+    r_copy.start()
+    t_copy = pltpu.make_async_copy(t_hbm, tg.at[x], t_sem)
+    t_copy.start()
     cut_low = (core == 1) & (x == 0)
     cut_high = (core == 0) & (x == last_x)
 
@@ -293,7 +315,7 @@
         return ring(k + len(PAIR), piece, piece, way)
 
     def first(k, step, way):
-        return ring(k, t_ref.at[core], tg.at[at(step), core], way)
+        return ring(k, t_hbm.at[core], tg.at[at(step), core], way)
 
     def across(step, side):
         piece = tg.at[at(step), side]
@@ -302,7 +324,7 @@
     opposite = (LEFT, RIGHT)
     for k, way in enumerate(WAYS):
         first(k, HERE, way).start()
-    tg[x] = t_ref[...]
+    r_copy.wait()
     rt[...] = r_ref[...].T
     lane = lax.broadcasted_iota(jnp.int32, (blk, LANES), 1)
     low = jnp.where(cut_low, half_tile, 0)
@@ -333,6 +355,7 @@
         across(opposite[k], core).start()
     lax.fori_loop(FAR, SIDE, student_logits, 0)
     each_ht(lambda copy: copy.wait())
+    t_copy.wait()
 
     def teacher_logits(i, _):
         for step, turn in ((RIGHT, 1), (LEFT, 2), (FAR, 3)):
@@ -427,15 +450,15 @@
         functools.partial(heads_kernel, kl_coef, chunk),
         out_shape=(jax.ShapeDtypeStruct((d_stud, cols), F32), jax.ShapeDtypeStruct((n_all, d_stud), F32),
                    jax.ShapeDtypeStruct((SUBS, LANES), F32)),
-        in_specs=[IN_VMEM, IN_VMEM, IN_HBM, IN_HBM],
+        in_specs=[IN_HBM] * SIDE,
         out_specs=(IN_HBM, IN_VMEM, IN_VMEM),
         scratch_shapes=[
-            v((SIDE, rows, n_tok, d_model), BF16), v((d_stud, n_all), BF16), v((cols, d_model), BF16), v((d_stud, cols), BF16),
+            v((n_all, d_stud), BF16), v((SIDE, rows, n_tok, d_model), BF16), v((d_stud, n_all), BF16), v((cols, d_model), BF16), v((d_stud, cols), BF16),
             v((SIDE, blk, cols), F32), v((SIDE, blk, cols), F32),
             v((len(PAIR), SIDE, blk, LANES), F32), v((len(PAIR), SIDE, blk, LANES), F32),
             v((SUBS, n_all), F32), v((n_peers + 1, SUBS, n_all), F32), v((n_all, LANES), F32),
             v((n_all, chunk), BF16),
-            DMA, DMA, DMA((SIDE,)), DMA((SIDE,)), DMA(hops), DMA(hops), DMA((n_peers,)), DMA((n_peers,)), DMA((len(PAIR),)),
+            DMA, DMA, DMA, DMA, DMA((SIDE,)), DMA((SIDE,)), DMA(hops), DMA(hops), DMA((n_peers,)), DMA((n_peers,)), DMA((len(PAIR),)),
         ],
         compiler_params=pltpu.CompilerParams(collective_id=collective_id, has_side_effects=True, vmem_limit_bytes=63 * MIB),
         cost_estimate=pl.CostEstimate(flops=d_model * n_all * cols, bytes_accessed=d_model * cols, transcendentals=0),
@@ -444,8 +467,9 @@
 
 
 class RingSum:
-    def __init__(self, coords, core, src, dims, order, lanes, bufs):
+    def __init__(self, coords, core, src, dims, order, lanes, bufs, loads=None):
         self.coords, self.core, self.order, self.lanes = coords, core, order, lanes
+        self.loads = src if loads is None else loads
         self.phases = []
         for axis, (half, full, mid, send, recv) in zip(order, bufs):
             self.phases.append((src, dims, axis, half, full, mid, send, recv))
@@ -479,6 +503,10 @@
         lead.insert(dims.index(axis), at)
         base = self.lanes if k == 0 else 0
         return src, tuple(lead) + (slice(None), pl.ds(base + lo, n))
+
+    def held(self, k, at, side):
+        src, idx = self.pick(k, at, side)
+        return (src if k else self.loads), idx
 
     def copy(self, k, turn, d):
         _, _, axis, half, full, _, send, recv = self.phases[k]
@@ -506,7 +534,7 @@
         _, _, axis, half, _, _, _, _ = self.phases[k]
         for d in PAIR:
             self.copy(k, 0, d).wait_recv()
-            ref, idx = self.pick(k, self.place(axis, WAYS[d]), d)
+            ref, idx = self.held(k, self.place(axis, WAYS[d]), d)
             n = self.split(k, d)[1][1]
             half[d, ..., :n] = half[d, ..., :n] + ref[idx]
             self.copy(k, len(PAIR), d).start()
@@ -516,7 +544,7 @@
         for d in PAIR:
             for turn in (1, len(PAIR)):
                 self.copy(k, turn, d).wait_recv()
-        ref, idx = self.pick(k, self.coords[axis], None)
+        ref, idx = self.held(k, self.coords[axis], None)
         mid[...] = ref[idx] + full[0] + full[1]
 
     def drain(self):
@@ -540,11 +568,16 @@
 
 
 def reduce_kernel(feat_coef, kl_coef, small_parts,
-                  dw, dx_ref, feat_a, feat_b, xs_ref, gs_ref, ups_ref, dns_ref, proj_ref, kl_ref,
-                  own, small, got, part_in, swap_send, swap_recv, in_send, in_recv, *bufs):
+                  dw_hbm, feat_a_hbm, feat_b_hbm, xs_hbm, gs_hbm, ups_hbm, dns_hbm, proj_hbm, dx_ref, kl_ref,
+                  own, dw, feat_a, feat_b, xs_ref, gs_ref, ups_ref, dns_ref, proj_ref, in_sems, small, got, part_in, swap_send, swap_recv, in_send, in_recv, *bufs):
     coords = chip_coords()
     core = lax.axis_index('tp')
     peer = device(coords, 1 - core)
+    loads = [pltpu.make_async_copy(src, dst, in_sems.at[i]) for i, (src, dst) in enumerate((
+        (dw_hbm, dw), (feat_a_hbm, feat_a), (feat_b_hbm, feat_b), (xs_hbm, xs_ref), (gs_hbm, gs_ref), (ups_hbm, ups_ref),
+        (dns_hbm, dns_ref), (proj_hbm, proj_ref)))]
+    for copy in loads[::-1]:
+        copy.start()
     greet(near_targets(coords, core))
     cols = dw.shape[-1]
     bufs = list(bufs)
@@ -554,13 +587,15 @@
         del bufs[:5 * n]
         return out
 
-    head_jobs = [RingSum(coords, core, dw, (Y, Z), order, k * (cols // 2), take(2)) for k, order in enumerate(((Y, Z), (Z, Y)))]
+    head_jobs = [RingSum(coords, core, dw_hbm, (Y, Z), order, k * (cols // 2), take(2), dw) for k, order in enumerate(((Y, Z), (Z, Y)))]
     in_job = RingSum(coords, core, part_in, (X,), (X,), 0, take(1))
     for job in head_jobs:
         job.start(0)
     in_swap = remote(dx_ref.at[:, 1 - core], part_in, in_send, in_recv, peer)
     in_swap.start()
 
+    for copy in loads:
+        copy.wait()
     saved, _ = student_layers(xs_ref, gs_ref, ups_ref, dns_ref)
     in_swap.wait()
     part_in[...] = part_in[...] + dx_ref[:, core]
@@ -630,26 +665,26 @@
         small_jobs.append(RingSum(coords, core, got, AXES, order, lo, take(3)))
         lo += width
     first, rest = small_jobs[0], small_jobs[1:]
+    for job in head_jobs:
+        job.finish(0)
+        job.start(1)
     for step in order_in:
         swap(step).wait()
         cx = lax.rem(coords[X] + step, SIDE)
         got[cx] = got[cx] + small[core, cx]
         if step in (FAR, LEFT):
             first.start(0, PAIR[step == LEFT:][:1])
+    for job in head_jobs:
+        job.middle(1)
     for job in rest:
         job.start(0)
-    for job in head_jobs:
-        job.finish(0)
-        job.start(1)
     for job in small_jobs:
         job.middle(0)
     for job in head_jobs:
-        job.middle(1)
+        job.finish(1)
     for job in small_jobs:
         job.finish(0)
         job.start(1)
-    for job in head_jobs:
-        job.finish(1)
     for k in (1, 2):
         for job in small_jobs:
             job.middle(k)
@@ -679,7 +714,9 @@
     span = sum(small_parts) // len(PARTS)
     width = cols // 2
     xs_shape = x_stud.shape
-    scratch = [pltpu.VMEM((len(PAIR), SIDE, SIDE, SIDE, SUBS, sum(small_parts)), F32),
+    args = (dw, *feats, x_stud, gain_s, w_up_s, w_down_s, proj_s)
+    scratch = [pltpu.VMEM(a.shape, a.dtype) for a in args]
+    scratch += [DMA((len(args),)), pltpu.VMEM((len(PAIR), SIDE, SIDE, SIDE, SUBS, sum(small_parts)), F32),
                pltpu.VMEM((SIDE, SIDE, SIDE, SUBS, sum(small_parts)), F32), pltpu.VMEM((SIDE,) + xs_shape, F32),
                DMA((SIDE,)), DMA((SIDE,)), DMA, DMA]
     for _ in PAIR:
@@ -690,13 +727,13 @@
     return pl.pallas_call(
         functools.partial(reduce_kernel, feat_coef, kl_coef, small_parts),
         out_shape=jax.ShapeDtypeStruct((len(PARTS), SUBS, cols + span + LANES), F32),
-        in_specs=[IN_VMEM] * 10,
+        in_specs=[IN_HBM] * len(args) + [IN_VMEM] * len(PAIR),
         out_specs=IN_VMEM,
         scratch_shapes=scratch,
-        compiler_params=pltpu.CompilerParams(collective_id=collective_id, has_side_effects=True, vmem_limit_bytes=62 * MIB),
+        compiler_params=pltpu.CompilerParams(collective_id=collective_id, has_side_effects=True, vmem_limit_bytes=63 * MIB),
         cost_estimate=pl.CostEstimate(flops=MIB * MIB, bytes_accessed=dw.size, transcendentals=0),
         name='reduce',
-    )(dw, dx, *feats, x_stud, gain_s, w_up_s, w_down_s, proj_s, kl_tiles)
+    )(*args, dx, kl_tiles)
 
 
 ALL = pl.ds(0, SIDE)

time: 399 us -> 387 us (0.970)
  Pallas kernels: 390 us -> 384 us
  local copies, waits for them, and re-layouts: 6.87 us -> 1.25 us
    pallas_call x1, Pallas kernels: 123 us -> 117 us  [teacher(): pl.pallas_call(functools.partial(teacher_kernel, feat_at, slots_w), out_s...]
    unnamed x14 -> x0, local copies, waits for them, and re-layouts: 5.61 us -> none
where the time goes in v4:
time: 387 us
  Pallas kernels  384 us (99%)
    pallas_call x1, Pallas kernels, gather_blocks(): pl.pallas_call(functools.partial(gather_kernel, cut), out_shape=pltpu.VME...  126 us
    pallas_call x1, Pallas kernels, teacher(): pl.pallas_call(functools.partial(teacher_kernel, feat_at, slots_w), out_s...  117 us
    pallas_call x1, Pallas kernels, reduce_grads(): pl.pallas_call(functools.partial(reduce_kernel, feat_coef, kl_coef, small...  69.9 us
    pallas_call x1, Pallas kernels, heads(): pl.pallas_call(functools.partial(heads_kernel, kl_coef, chunk), out_shape...  50.4 us
    pallas_call x1, Pallas kernels, place_blocks(): pl.pallas_call(functools.partial(place_kernel, n_head, lanes_u, lanes_p),...  19.7 us

profile of v4, /device:TPU:1, one launch (start us, length us, event | category | flops | bytes accessed | tf_op | source)
XLA Modules:
  0.0 386.9 jit_solution(8062369217905765243)
XLA Ops:
  0.6 117.2 %teacher.1 = (bf16[128,1024]{1,0:T(8,128)(2,1)}, bf16[128,1024]{1,0:T(8,128)(2,1)}, bf16[2,128,1024]{2,1,0:T(8,128)(2,1)}, bf16[4,2,128,384]{3,2,1,0:T(8,128)(2,1)}) custom-call(bf16[2,64,1024]{2,1,0:T(8,128)(2,1)} %x_hbm.1, bf16[128,384]{1,0:T(8,128)(2,1)} %bitcast.12, f32[2,384]{1,0:T(2,128)} %gs_hbm.3, bf16[2,384,1536]{2,1,0:T(8,128)(2,1)} %ups_hbm.3, ...), custom_call_target="tpu_custom_call" | custom-call | flops 68719476736 | bytes 268435456 | tf_op jit(solution)/shard_map/teacher/pallas_call | solution.py:233
  117.8 50.4 %heads.1 = (f32[384,3840]{1,0:T(8,128)}, f32[1024,384]{1,0:T(8,128)}, f32[8,128]{1,0:T(8,128)}) custom-call(bf16[2,128,1024]{2,1,0:T(8,128)(2,1)} %get-tuple-element.18.t_hbm, bf16[1024,384]{1,0:T(8,128)(2,1)} %bitcast.11, bf16[15296,1024]{1,0:T(8,128)(2,1)} %bitcast.10, bf16[384,30592]{1,0:T(8,128)(2,1)} %hs_hbm.1), custom_call_target="tpu_custom_call" | custom-call | flops 4026531840 | bytes 3932160 | tf_op jit(solution)/shard_map/heads/pallas_call | solution.py:449
  168.2 69.9 %reduce.2.own_ref = f32[3,8,4992]{2,1,0:T(8,128)} custom-call(f32[4,4,24,3840]{3,2,1,0:T(8,128)} %bitcast.16, bf16[128,1024]{1,0:T(8,128)(2,1)} %get-tuple-element.21.feat_a_hbm, bf16[128,1024]{1,0:T(8,128)(2,1)} %get-tuple-element.22.feat_b_hbm, bf16[128,384]{1,0:T(8,128)(2,1)} %bitcast.13, f32[2,384]{1,0:T(2,128)} %gs_hbm.3, ...), custom_call_target="tpu_custom_call" | custom-call | flops 1099511627776 | bytes 1474560 | tf_op jit(solution)/shard_map/reduce/pallas_call | solution.py:727
  238.2 126.5 %gather.1.full = f32[2,4,4,4,3,8,4992]{6,5,4,3,2,1,0:T(8,128)S(1)} custom-call(f32[3,8,4992]{2,1,0:T(8,128)} %reduce.2.own_ref), custom_call_target="tpu_custom_call" | custom-call | flops 1099511627776 | bytes 61341696 | tf_op jit(solution)/shard_map/gather/pallas_call | solution.py:849
  364.6 19.7 %place.1 = (f32[4,4,3,8,30592]{4,3,2,1,0:T(8,128)}, f32[4,4,3,2,8,1536]{5,4,3,2,1,0:T(8,128)}, f32[4,4,4,3,2,8,384]{6,5,4,3,2,1,0:T(8,128)}, f32[2,4,4,3,8,1024]{5,4,3,2,1,0:T(8,128)}, f32[8,128]{1,0:T(8,128)}) custom-call(f32[2,4,4,4,3,8,4992]{6,5,4,3,2,1,0:T(8,128)S(1)} %gather.1.full), custom_call_target="tpu_custom_call" | custom-call | tf_op jit(solution)/shard_map/place/pallas_call | solution.py:901
  384.4 1.3 slice_reduce_fusion
  385.7 1.3 reshape.41

commit v5 on v4

--- a/solution.py
+++ b/solution.py
@@ -255,10 +255,10 @@
 TEACH, STUD = PAIR
 
 
-def heads_kernel(kl_coef, chunk,
+def heads_kernel(kl_coef, chunk, strip,
                  t_hbm, r_hbm, ht_hbm, hs_hbm,
                  dw_hbm, dx, kl_ref,
-                 r_ref, tg, rt, ht, hs, zt, zs, mx, sm, st_send, st_all, lcol, grad,
+                 r_ref, tg, rt, ht, hs, zt, zs, mx, sm, st_send, st_all, lcol, grad_a, grad_b, dw_out,
                  ht_sem, hs_sem, t_sem, r_sem, ring_send, ring_recv, peer_send, peer_recv, st_send_sem, st_recv_sem, out_sem):
     coords = chip_coords()
     x = coords[X]
@@ -330,21 +330,31 @@
     low = jnp.where(cut_low, half_tile, 0)
     high = jnp.where(cut_high, half_tile, LANES)
 
-    def finish(kind, b, ref):
-        head, tail = lane_slice(0, LANES), lane_slice(n_tiles - 1, LANES)
-        ref[b, :, head] = jnp.where(lane >= low, ref[b, :, head], NEG)
-        ref[b, :, tail] = jnp.where(lane < high, ref[b, :, tail], NEG)
-        tiles = [lane_slice(k, LANES) for k in range(n_tiles)]
-        peak = functools.reduce(jnp.maximum, [ref[b, :, t] for t in tiles])
+    def logits(kind, b, ref, product):
+        peak = total = None
+        for c in range(cols // chunk):
+            lanes = lane_slice(c, chunk)
+            z = product(lanes)
+            tiles = [z[:, lane_slice(k, LANES)] for k in range(chunk // LANES)]
+            if c == 0:
+                tiles[0] = jnp.where(lane >= low, tiles[0], NEG)
+            if lanes.stop == cols:
+                tiles[-1] = jnp.where(lane < high, tiles[-1], NEG)
+            for k, tile in enumerate(tiles):
+                ref[b, :, lane_slice(c * len(tiles) + k, LANES)] = tile
+            top = functools.reduce(jnp.maximum, tiles if peak is None else [peak] + tiles)
+            sums = [jnp.exp(tile - top) for tile in tiles]
+            total = functools.reduce(jnp.add, sums if peak is None else [total * jnp.exp(peak - top)] + sums)
+            peak = top
         mx[kind, b] = peak
-        sm[kind, b] = functools.reduce(jnp.add, [jnp.exp(ref[b, :, t] - peak) for t in tiles])
+        sm[kind, b] = total
 
     def tokens(b):
         return pl.ds(pl.multiple_of(b * blk, blk), blk)
 
     def student_logits(b, _):
-        zs[b] = dot(r_ref[tokens(b), :], hs[...])
-        finish(STUD, b, zs)
+        states = r_ref[tokens(b), :]
+        logits(STUD, b, zs, lambda lanes: dot(states, hs[:, lanes]))
         return 0
 
     hs_copy.wait()
@@ -361,15 +371,15 @@
         for step, turn in ((RIGHT, 1), (LEFT, 2), (FAR, 3)):
             @pl.when(i == turn)
             def _():
-                if step == RIGHT:
+                if step == LEFT:
                     for k, way in enumerate(WAYS):
                         onward(k, FAR, way).wait_recv()
                     across(FAR, core).start()
                 across(step, 1 - core).wait_recv()
 
         b = at(jnp.where(i < FAR, i, SIDE + 1 - i))
-        zt[b] = dot_right_t(tg[b].reshape(blk, d_model), ht[...])
-        finish(TEACH, b, zt)
+        states = tg[b].reshape(blk, d_model)
+        logits(TEACH, b, zt, lambda lanes: dot_right_t(states, ht[lanes, :]))
         return 0
 
     lax.fori_loop(0, SIDE, teacher_logits, 0)
@@ -402,43 +412,61 @@
     kl_ref[...] = jnp.zeros_like(kl_ref)
     dx[...] = jnp.zeros_like(dx)
 
-    def grad_step(j, _):
-        lanes = pl.ds(pl.multiple_of(j * chunk, LANES), chunk)
-
-        def block(b, _):
-            tok = tokens(b)
-            log_pt = zt[b, :, lanes] - lcol[tok, TEACH:TEACH + 1]
-            log_ps = zs[b, :, lanes] - lcol[tok, STUD:STUD + 1]
+    n_steps = cols // chunk
+
+    def lanes_of(j):
+        return pl.ds(pl.multiple_of(j * chunk, LANES), chunk)
+
+    def logit_grads(j, dst):
+        lanes = lanes_of(j)
+        total = kl_ref[...]
+        for i in range(n_all // strip):
+            b, k = divmod(i, blk // strip)
+            tok, row = lane_slice(i, strip), lane_slice(k, strip)
+            log_pt = zt[b, row, lanes] - lcol[tok, TEACH:TEACH + 1]
+            log_ps = zs[b, row, lanes] - lcol[tok, STUD:STUD + 1]
             pt = jnp.exp(log_pt)
-            grad[tok, :] = (kl_coef * (jnp.exp(log_ps) - pt)).astype(BF16)
+            dst[tok, :] = (kl_coef * (jnp.exp(log_ps) - pt)).astype(BF16)
             kl = pt * (log_pt - log_ps)
             kl = functools.reduce(jnp.add, [kl[:, lane_slice(k, LANES)] for k in range(chunk // LANES)])
-            kl_ref[...] += functools.reduce(jnp.add, [kl[lane_slice(k, SUBS)] for k in range(blk // SUBS)])
-            return 0
-
-        lax.fori_loop(0, SIDE, block, 0)
-        dw = dot(rt[...], grad[...])
-        zt[0, :, lanes] = dw[:blk]
-        zt[1, :d_stud - blk, lanes] = dw[blk:]
-        dx[...] += dot_right_t(grad[...], hs[:, lanes])
+            total = total + functools.reduce(jnp.add, [kl[lane_slice(k, SUBS)] for k in range(strip // SUBS)])
+        kl_ref[...] = total
+
+    def out_copy(j):
+        return pltpu.make_async_copy(dw_out, dw_hbm.at[:, lanes_of(j)], out_sem)
+
+    def products(j, src):
+        dw_out[...] = dot(rt[...], src[...])
+        out_copy(j).start()
+        dx[...] += dot_right_t(src[...], hs[:, lanes_of(j)])
+
+    def two_steps(i, _):
+        j = 2 * i
+
+        @pl.when(i > 0)
+        def _():
+            out_copy(j - 1).wait()
+
+        logit_grads(j + 1, grad_b)
+        products(j, grad_a)
+        out_copy(j).wait()
+        logit_grads(j + 2, grad_a)
+        products(j + 1, grad_b)
         return 0
 
-    lax.fori_loop(0, cols // chunk, grad_step, 0)
-    outs = [pltpu.make_async_copy(zt.at[k, pl.ds(0, n)], dw_hbm.at[pl.ds(k * blk, n)], out_sem.at[k])
-            for k, n in enumerate((blk, d_stud - blk))]
-    for copy in outs:
-        copy.start()
-
+    logit_grads(0, grad_a)
+    lax.fori_loop(0, n_steps // 2, two_steps, 0)
+    out_copy(n_steps - 2).wait()
+    products(n_steps - 1, grad_a)
     for k, way in enumerate(WAYS):
         first(k, HERE, way).wait_send()
         onward(k, opposite[k], way).wait_send()
     for step in (RIGHT, FAR, LEFT):
         across(step, core).wait_send()
-    for copy in outs:
-        copy.wait()
-
-
-def heads(states, stud_all, head_t, head_s, kl_coef, collective_id, chunk=768):
+    out_copy(n_steps - 1).wait()
+
+
+def heads(states, stud_all, head_t, head_s, kl_coef, collective_id, chunk=768, strip=16):
     rows, n_tok, d_model = states.shape
     n_all, d_stud = stud_all.shape
     cols = -(-head_t.shape[1] // (LANES * SIDE)) * LANES
@@ -447,7 +475,7 @@
     v = pltpu.VMEM
     hops = (SIDE - 1,)
     return pl.pallas_call(
-        functools.partial(heads_kernel, kl_coef, chunk),
+        functools.partial(heads_kernel, kl_coef, chunk, strip),
         out_shape=(jax.ShapeDtypeStruct((d_stud, cols), F32), jax.ShapeDtypeStruct((n_all, d_stud), F32),
                    jax.ShapeDtypeStruct((SUBS, LANES), F32)),
         in_specs=[IN_HBM] * SIDE,
@@ -457,8 +485,8 @@
             v((SIDE, blk, cols), F32), v((SIDE, blk, cols), F32),
             v((len(PAIR), SIDE, blk, LANES), F32), v((len(PAIR), SIDE, blk, LANES), F32),
             v((SUBS, n_all), F32), v((n_peers + 1, SUBS, n_all), F32), v((n_all, LANES), F32),
-            v((n_all, chunk), BF16),
-            DMA, DMA, DMA, DMA, DMA((SIDE,)), DMA((SIDE,)), DMA(hops), DMA(hops), DMA((n_peers,)), DMA((n_peers,)), DMA((len(PAIR),)),
+            v((n_all, chunk), BF16), v((n_all, chunk), BF16), v((d_stud, chunk), F32),
+            DMA, DMA, DMA, DMA, DMA((SIDE,)), DMA((SIDE,)), DMA(hops), DMA(hops), DMA((n_peers,)), DMA((n_peers,)), DMA,
         ],
         compiler_params=pltpu.CompilerParams(collective_id=collective_id, has_side_effects=True, vmem_limit_bytes=63 * MIB),
         cost_estimate=pl.CostEstimate(flops=d_model * n_all * cols, bytes_accessed=d_model * cols, transcendentals=0),
@@ -576,7 +604,8 @@
     loads = [pltpu.make_async_copy(src, dst, in_sems.at[i]) for i, (src, dst) in enumerate((
         (dw_hbm, dw), (feat_a_hbm, feat_a), (feat_b_hbm, feat_b), (xs_hbm, xs_ref), (gs_hbm, gs_ref), (ups_hbm, ups_ref),
         (dns_hbm, dns_ref), (proj_hbm, proj_ref)))]
-    for copy in loads[::-1]:
+    dw_load = loads.pop(0)
+    for copy in loads + [dw_load]:
         copy.start()
     greet(near_targets(coords, core))
     cols = dw.shape[-1]
@@ -613,6 +642,16 @@
         part, q = divmod(g, per // per_p)
         small[keep, chip_x, y, z, :, part * span + base + q * lanes:part * span + base + q * lanes + lanes] = value
 
+    half_side = SIDE // n_feat
+    swaps = []
+
+    def swap(k, rows_y, base, lanes):
+        for p in PARTS:
+            window = (slice(None), rows_y, slice(None), slice(None), pl.ds(p * span + base, lanes))
+            copy = remote(small.at[(1 - core,) + window], got.at[window], swap_send.at[k, p], swap_recv.at[k, p], peer)
+            copy.start()
+            swaps.append((copy, window))
+
     for j in range(n_feat):
         proj_in = saved[j][5].astype(BF16)
         err = dot(proj_in, proj_ref[j]) - feats[j][...].astype(F32)
@@ -625,7 +664,9 @@
             for cx in range(SIDE):
                 put(j, cx, i, per_p, two * lanes_u, lanes_p, g_proj[lane_slice(i, SUBS), lane_slice(cx, lanes_p)])
         out_grads.append(dot_right_t(err_grad, proj_ref[j]))
+    swap(n_feat, slice(None), two * lanes_u, lanes_p)
     in_job.middle(0)
+    dw_load.wait()
     for job in head_jobs:
         job.middle(0)
     in_job.finish(0)
@@ -639,45 +680,36 @@
         g_down = dot_left_t(act, resid_bf)
         n_down = d_mid // SUBS
         for i in range(n_down):
-            cx, rest = divmod(j * n_down + i, n_feat * n_down // SIDE)
-            put(1, cx, rest, per_up, 0, lanes_u, g_down[lane_slice(i, SUBS), :])
+            cx, rest = divmod(i, groups)
+            put(1, cx, j * groups + rest, per_up, 0, lanes_u, g_down[lane_slice(i, SUBS), :])
         pre_grad = (gelu_slope(pre) * dot_right_t(resid_bf, dns_ref[j])).astype(BF16)
         g_up = dot_left_t(normed, pre_grad)
         for i in range(groups):
             for cx in range(SIDE):
                 put(0, cx, j * groups + i, per_up, 0, lanes_u, g_up[lane_slice(i, SUBS), lane_slice(cx, lanes_u)])
+        swap(j, pl.ds(half_side * j, half_side), 0, two * lanes_u)
         norm_grad = dot_right_t(pre_grad, ups_ref[j])
         g_gain = jnp.sum(norm_grad * unit, axis=0, keepdims=True)
         gain_rows = [g_gain[:, lane_slice(k, LANES)] for k in range(d_in // LANES)] + gain_rows
         if j > 0:
             resid_grad = resid_grad + rms_back(unit, inv, norm_grad * gs_ref[j:j + 1, :])
 
-    def swap(step):
-        cx = lax.rem(coords[X] + step, SIDE)
-        return remote(small.at[1 - core, cx], got.at[cx], swap_send.at[step], swap_recv.at[step], peer)
-
-    order_in = (FAR, RIGHT, LEFT, HERE)
-    for step in order_in:
-        swap(step).start()
     lo = 0
     small_jobs = []
     for order, width in zip(ORDERS, small_parts):
         small_jobs.append(RingSum(coords, core, got, AXES, order, lo, take(3)))
         lo += width
-    first, rest = small_jobs[0], small_jobs[1:]
+    for copy, window in swaps:
+        copy.wait()
+        got[window] = got[window] + small[(core,) + window]
+    for turn in PAIR:
+        for job in small_jobs:
+            job.start(0, (turn,))
     for job in head_jobs:
         job.finish(0)
         job.start(1)
-    for step in order_in:
-        swap(step).wait()
-        cx = lax.rem(coords[X] + step, SIDE)
-        got[cx] = got[cx] + small[core, cx]
-        if step in (FAR, LEFT):
-            first.start(0, PAIR[step == LEFT:][:1])
     for job in head_jobs:
         job.middle(1)
-    for job in rest:
-        job.start(0)
     for job in small_jobs:
         job.middle(0)
     for job in head_jobs:
@@ -718,7 +750,7 @@
     scratch = [pltpu.VMEM(a.shape, a.dtype) for a in args]
     scratch += [DMA((len(args),)), pltpu.VMEM((len(PAIR), SIDE, SIDE, SIDE, SUBS, sum(small_parts)), F32),
                pltpu.VMEM((SIDE, SIDE, SIDE, SUBS, sum(small_parts)), F32), pltpu.VMEM((SIDE,) + xs_shape, F32),
-               DMA((SIDE,)), DMA((SIDE,)), DMA, DMA]
+               DMA((SIDE, SIDE)), DMA((SIDE, SIDE)), DMA, DMA]
     for _ in PAIR:
         scratch += RingSum.shapes((Y, Z), (Y, Z), rows, width)
     scratch += RingSum.shapes((X,), (X,), *xs_shape)
@@ -859,10 +891,11 @@
 
 
 def place_kernel(n_head, lanes_u, lanes_p,
-                 full, head, up, down, proj, total,
-                 edge, head_sem, edge_sem, wide_sem, narrow_sem):
+                 full, head, up, down, proj, gain, loss,
+                 total, edge, head_sem, edge_sem, up_sem, down_sem, narrow_sem):
     last_x = SIDE - 1
     per = up.shape[3]
+    n_feat, _, half_side = down.shape[:3]
     copy = pltpu.make_async_copy
     narrow_at = n_head + per * lanes_u
     copies = []
@@ -874,8 +907,13 @@
             at = (c * SIDE + x) * n_head - c * LANES
             copies.append(copy(src.at[:, :, :, :, pl.ds(lo, hi - lo)], head.at[:, :, :, :, pl.ds(at + lo, hi - lo)], head_sem.at[c, x]))
             for q in range(per):
-                dst = down.at[x, :, :, :, q] if c else up.at[:, :, :, q, :, pl.ds(x * lanes_u, lanes_u)]
-                copies.append(copy(src.at[:, :, :, :, pl.ds(n_head + q * lanes_u, lanes_u)], dst, wide_sem.at[c, x, q]))
+                lanes = pl.ds(n_head + q * lanes_u, lanes_u)
+                if c:
+                    for j in range(n_feat):
+                        copies.append(copy(src.at[pl.ds(j * half_side, half_side), :, :, :, lanes], down.at[j, x, :, :, :, q],
+                                           down_sem.at[x, q, j]))
+                else:
+                    copies.append(copy(src.at[:, :, :, :, lanes], up.at[:, :, :, q, :, pl.ds(x * lanes_u, lanes_u)], up_sem.at[x, q]))
             copies.append(copy(src.at[:, :, :, :, pl.ds(narrow_at, lanes_p)], proj.at[c, :, :, :, :, pl.ds(x * lanes_p, lanes_p)],
                                narrow_sem.at[c, x]))
     for one in copies:
@@ -885,25 +923,32 @@
     edge_copy.start()
     tiles = full[:, :, :, :, 0, :, narrow_at + lanes_p:narrow_at + lanes_p + LANES]
     total[...] = jnp.sum(tiles.reshape(-1, SUBS, LANES), axis=0)
+    rows = gain.shape[1] // LANES
+    for j in range(n_feat):
+        for k in range(rows):
+            gain[j:j + 1, lane_slice(k, LANES)] = total[j * rows + k:j * rows + k + 1, :]
+    loss[...] = jnp.sum(total[n_feat * rows:n_feat * rows + 1, :], axis=-1, keepdims=True)
     edge_copy.wait()
     for one in copies:
         one.wait()
 
 
-def place_blocks(full, n_head, lanes_u, lanes_p, vocab):
+def place_blocks(full, n_head, lanes_u, lanes_p, vocab, gain_shape):
     n_part, subs, _ = full.shape[4:]
     per = len(PAIR)
+    n_feat = gain_shape[0]
     pair = (len(PAIR),)
     owners = pair + (SIDE,)
     yz = (SIDE, SIDE)
-    shapes = (yz + (n_part, subs, vocab), yz + (n_part, per, subs, SIDE * lanes_u), (SIDE,) + yz + (n_part, per, subs, lanes_u),
-              pair + yz + (n_part, subs, SIDE * lanes_p), (subs, LANES))
+    shapes = (yz + (n_part, subs, vocab), yz + (n_part, per, subs, SIDE * lanes_u), (n_feat, SIDE, SIDE // n_feat, SIDE, n_part, per, subs, lanes_u),
+              pair + yz + (n_part, subs, SIDE * lanes_p), gain_shape, (1, 1))
     return pl.pallas_call(
         functools.partial(place_kernel, n_head, lanes_u, lanes_p),
         out_shape=tuple(jax.ShapeDtypeStruct(s, F32) for s in shapes),
         in_specs=[IN_VMEM],
-        out_specs=(IN_HBM,) * SIDE + (IN_VMEM,),
-        scratch_shapes=[pltpu.VMEM(yz + (n_part, subs, LANES), F32), DMA(owners), DMA, DMA(owners + (per,)), DMA(owners)],
+        out_specs=(IN_HBM,) * SIDE + (IN_VMEM, IN_VMEM),
+        scratch_shapes=[pltpu.VMEM((subs, LANES), F32), pltpu.VMEM(yz + (n_part, subs, LANES), F32), DMA(owners), DMA,
+                        DMA((SIDE, per)), DMA((SIDE, per, n_feat)), DMA(owners)],
         compiler_params=pltpu.CompilerParams(has_side_effects=True, vmem_limit_bytes=MIB),
         name='place',
     )(pltpu.with_memory_space_constraint(full, pltpu.VMEM))
@@ -926,9 +971,8 @@
         own = reduce_grads(head_part.reshape(SIDE, SIDE, -1, cols), in_part.reshape((SIDE, -1) + xs.shape), (feat_one, feat_two), xs, gain_s, w_up_s, w_down_s,
                            proj_s, kl_tiles, feat_coef, kl_coef, 2)
         blocks = gather_blocks(own, 20 * LANES, 3)
-        head_grad, up, down, proj, total = place_blocks(blocks, cols, d_mid // SIDE, d_teach // SIDE, head_s.shape[1])
-        n_gain = n_feat * d_in // LANES
-        return (jnp.sum(total[n_gain]), up.reshape(w_up_s.shape), down.reshape(w_down_s.shape), total[:n_gain].reshape(gain_s.shape),
+        head_grad, up, down, proj, gain, loss = place_blocks(blocks, cols, d_mid // SIDE, d_teach // SIDE, head_s.shape[1], gain_s.shape)
+        return (loss.reshape(()), up.reshape(w_up_s.shape), down.reshape(w_down_s.shape), gain,
                 proj.reshape(proj_s.shape), head_grad.reshape(head_s.shape))
 
     in_specs = (P('dp', 'tp', None), P(('dp', 'tp'), None, None), P(None, None, 'tp'), P(None, 'tp', None),

time: 387 us -> 377 us (0.974)
  Pallas kernels: 384 us -> 376 us
    pallas_call x1, Pallas kernels: 50.4 us -> 44.9 us  [heads(): pl.pallas_call(functools.partial(heads_kernel, kl_coef, chunk, strip), ou...]
where the time goes in v5:
time: 377 us
  Pallas kernels  376 us (100%)
    pallas_call x1, Pallas kernels, gather_blocks(): pl.pallas_call(functools.partial(gather_kernel, cut), out_shape=pltpu.VME...  127 us
    pallas_call x1, Pallas kernels, teacher(): pl.pallas_call(functools.partial(teacher_kernel, feat_at, slots_w), out_s...  117 us
    pallas_call x1, Pallas kernels, reduce_grads(): pl.pallas_call(functools.partial(reduce_kernel, feat_coef, kl_coef, small...  67.7 us
    pallas_call x1, Pallas kernels, heads(): pl.pallas_call(functools.partial(heads_kernel, kl_coef, chunk, strip), ou...  44.9 us
    pallas_call x1, Pallas kernels, place_blocks(): pl.pallas_call(functools.partial(place_kernel, n_head, lanes_u, lanes_p),...  19.8 us

profile of v5, /device:TPU:1, one launch (start us, length us, event | category | flops | bytes accessed | tf_op | source)
XLA Modules:
  0.0 376.9 jit_solution(8624694793612242659)
XLA Ops:
  0.6 117.2 %teacher.1 = (bf16[128,1024]{1,0:T(8,128)(2,1)}, bf16[128,1024]{1,0:T(8,128)(2,1)}, bf16[2,128,1024]{2,1,0:T(8,128)(2,1)}, bf16[4,2,128,384]{3,2,1,0:T(8,128)(2,1)}) custom-call(bf16[2,64,1024]{2,1,0:T(8,128)(2,1)} %x_hbm.1, bf16[128,384]{1,0:T(8,128)(2,1)} %bitcast.12, f32[2,384]{1,0:T(2,128)} %gs_hbm.3, bf16[2,384,1536]{2,1,0:T(8,128)(2,1)} %ups_hbm.3, ...), custom_call_target="tpu_custom_call" | custom-call | flops 68719476736 | bytes 268435456 | tf_op jit(solution)/shard_map/teacher/pallas_call | solution.py:233
  117.8 44.9 %heads.1 = (f32[384,3840]{1,0:T(8,128)}, f32[1024,384]{1,0:T(8,128)}, f32[8,128]{1,0:T(8,128)}) custom-call(bf16[2,128,1024]{2,1,0:T(8,128)(2,1)} %get-tuple-element.19.t_hbm, bf16[1024,384]{1,0:T(8,128)(2,1)} %bitcast.11, bf16[15296,1024]{1,0:T(8,128)(2,1)} %bitcast.10, bf16[384,30592]{1,0:T(8,128)(2,1)} %hs_hbm.1), custom_call_target="tpu_custom_call" | custom-call | flops 4026531840 | bytes 3932160 | tf_op jit(solution)/shard_map/heads/pallas_call | solution.py:477
  162.7 67.7 %reduce.1.own_ref = f32[3,8,4992]{2,1,0:T(8,128)} custom-call(f32[4,4,24,3840]{3,2,1,0:T(8,128)} %bitcast.15, bf16[128,1024]{1,0:T(8,128)(2,1)} %get-tuple-element.22.feat_a_hbm, bf16[128,1024]{1,0:T(8,128)(2,1)} %get-tuple-element.23.feat_b_hbm, bf16[128,384]{1,0:T(8,128)(2,1)} %bitcast.13, f32[2,384]{1,0:T(2,128)} %gs_hbm.3, ...), custom_call_target="tpu_custom_call" | custom-call | flops 1099511627776 | bytes 1474560 | tf_op jit(solution)/shard_map/reduce/pallas_call | solution.py:759
  230.4 126.5 %gather.1.full = f32[2,4,4,4,3,8,4992]{6,5,4,3,2,1,0:T(8,128)S(1)} custom-call(f32[3,8,4992]{2,1,0:T(8,128)} %reduce.1.own_ref), custom_call_target="tpu_custom_call" | custom-call | flops 1099511627776 | bytes 61341696 | tf_op jit(solution)/shard_map/gather/pallas_call | solution.py:881
  356.9 19.8 %place.1 = (f32[4,4,3,8,30592]{4,3,2,1,0:T(8,128)}, f32[4,4,3,2,8,1536]{5,4,3,2,1,0:T(8,128)}, f32[2,4,2,4,3,2,8,384]{7,6,5,4,3,2,1,0:T(8,128)}, f32[2,4,4,3,8,1...) custom-call(f32[2,4,4,4,3,8,4992]{6,5,4,3,2,1,0:T(8,128)S(1)} %gather.1.full), custom_call_target="tpu_custom_call" | custom-call | tf_op jit(solution)/shard_map/place/pallas_call | solution.py:945

commit v6 on v5

--- a/solution.py
+++ b/solution.py
@@ -130,7 +130,6 @@
     peer = device(coords, 1 - me)
     n_layers = gain_ref.shape[0]
     rows, seq_half, d_model = x_hbm.shape
-    d_ff = wu.shape[-1]
 
     def up_copy(layer, slot):
         return pltpu.make_async_copy(wup_hbm.at[layer], wu.at[slot], usem.at[slot])
@@ -191,11 +190,8 @@
             if first:
                 up_copy(layer, ws).wait()
                 down_copy(layer, ws).wait()
-            halves = []
-            for piece in (slice(None, d_ff // 2), slice(d_ff // 2, None)):
-                act = gelu_of_half(dot(nrm[...], wu[ws, :, piece])).astype(BF16)
-                halves.append(dot(act, wd[ws, piece, :]))
-            part[ck, slot] = halves[0] + halves[1]
+            act = gelu_of_half(dot(nrm[...], wu[ws])).astype(BF16)
+            part[ck, slot] = dot(act, wd[ws])
             p_copy(ck, slot).start()
             if last:
                 @pl.when(layer + slots_w < n_layers)
@@ -623,12 +619,13 @@
     in_swap = remote(dx_ref.at[:, 1 - core], part_in, in_send, in_recv, peer)
     in_swap.start()
 
+    in_swap.wait()
+    part_in[...] = part_in[...] + dx_ref[:, core]
+    in_job.start(0)
+
     for copy in loads:
         copy.wait()
     saved, _ = student_layers(xs_ref, gs_ref, ups_ref, dns_ref)
-    in_swap.wait()
-    part_in[...] = part_in[...] + dx_ref[:, core]
-    in_job.start(0)
     feats = (feat_a, feat_b)
     n_feat, d_in, d_mid = ups_ref.shape
     groups, yz, per_up, lanes_u, lanes_p, per_p, span = small_places(n_feat, d_in, d_mid, proj_ref.shape[-1])
@@ -666,10 +663,10 @@
         out_grads.append(dot_right_t(err_grad, proj_ref[j]))
     swap(n_feat, slice(None), two * lanes_u, lanes_p)
     in_job.middle(0)
+    in_job.finish(0)
     dw_load.wait()
     for job in head_jobs:
         job.middle(0)
-    in_job.finish(0)
     out_grads[-1] = out_grads[-1] + in_job.phases[-1][5][...]
     resid_grad = None
     for j in reversed(range(n_feat)):

time: 377 us -> 376 us (level)
  no operation moved by 1% of the time
where the time goes in v6:
time: 376 us
  Pallas kernels  375 us (100%)
    pallas_call x1, Pallas kernels, gather_blocks(): pl.pallas_call(functools.partial(gather_kernel, cut), out_shape=pltpu.VME...  126 us
    pallas_call x1, Pallas kernels, teacher(): pl.pallas_call(functools.partial(teacher_kernel, feat_at, slots_w), out_s...  117 us
    pallas_call x1, Pallas kernels, reduce_grads(): pl.pallas_call(functools.partial(reduce_kernel, feat_coef, kl_coef, small...  67.7 us
    pallas_call x1, Pallas kernels, heads(): pl.pallas_call(functools.partial(heads_kernel, kl_coef, chunk, strip), ou...  44.8 us
    pallas_call x1, Pallas kernels, place_blocks(): pl.pallas_call(functools.partial(place_kernel, n_head, lanes_u, lanes_p),...  19.8 us

profile of v6, /device:TPU:1, one launch (start us, length us, event | category | flops | bytes accessed | tf_op | source)
XLA Modules:
  0.0 376.0 jit_solution(6925660187076724152)
XLA Ops:
  0.6 116.6 %teacher.1 = (bf16[128,1024]{1,0:T(8,128)(2,1)}, bf16[128,1024]{1,0:T(8,128)(2,1)}, bf16[2,128,1024]{2,1,0:T(8,128)(2,1)}, bf16[4,2,128,384]{3,2,1,0:T(8,128)(2,1)}) custom-call(bf16[2,64,1024]{2,1,0:T(8,128)(2,1)} %x_hbm.1, bf16[128,384]{1,0:T(8,128)(2,1)} %bitcast.12, f32[2,384]{1,0:T(2,128)} %gs_hbm.3, bf16[2,384,1536]{2,1,0:T(8,128)(2,1)} %ups_hbm.3, ...), custom_call_target="tpu_custom_call" | custom-call | flops 68719476736 | bytes 268435456 | tf_op jit(solution)/shard_map/teacher/pallas_call | solution.py:229
  117.3 44.8 %heads.1 = (f32[384,3840]{1,0:T(8,128)}, f32[1024,384]{1,0:T(8,128)}, f32[8,128]{1,0:T(8,128)}) custom-call(bf16[2,128,1024]{2,1,0:T(8,128)(2,1)} %get-tuple-element.19.t_hbm, bf16[1024,384]{1,0:T(8,128)(2,1)} %bitcast.11, bf16[15296,1024]{1,0:T(8,128)(2,1)} %bitcast.10, bf16[384,30592]{1,0:T(8,128)(2,1)} %hs_hbm.1), custom_call_target="tpu_custom_call" | custom-call | flops 4026531840 | bytes 3932160 | tf_op jit(solution)/shard_map/heads/pallas_call | solution.py:473
  162.1 67.7 %reduce.1.own_ref = f32[3,8,4992]{2,1,0:T(8,128)} custom-call(f32[4,4,24,3840]{3,2,1,0:T(8,128)} %bitcast.15, bf16[128,1024]{1,0:T(8,128)(2,1)} %get-tuple-element.22.feat_a_hbm, bf16[128,1024]{1,0:T(8,128)(2,1)} %get-tuple-element.23.feat_b_hbm, bf16[128,384]{1,0:T(8,128)(2,1)} %bitcast.13, f32[2,384]{1,0:T(2,128)} %gs_hbm.3, ...), custom_call_target="tpu_custom_call" | custom-call | flops 1099511627776 | bytes 1474560 | tf_op jit(solution)/shard_map/reduce/pallas_call | solution.py:756
  229.8 126.3 %gather.1.full = f32[2,4,4,4,3,8,4992]{6,5,4,3,2,1,0:T(8,128)S(1)} custom-call(f32[3,8,4992]{2,1,0:T(8,128)} %reduce.1.own_ref), custom_call_target="tpu_custom_call" | custom-call | flops 1099511627776 | bytes 61341696 | tf_op jit(solution)/shard_map/gather/pallas_call | solution.py:878
  356.1 19.8 %place.1 = (f32[4,4,3,8,30592]{4,3,2,1,0:T(8,128)}, f32[4,4,3,2,8,1536]{5,4,3,2,1,0:T(8,128)}, f32[2,4,2,4,3,2,8,384]{7,6,5,4,3,2,1,0:T(8,128)}, f32[2,4,4,3,8,1...) custom-call(f32[2,4,4,4,3,8,4992]{6,5,4,3,2,1,0:T(8,128)S(1)} %gather.1.full), custom_call_target="tpu_custom_call" | custom-call | tf_op jit(solution)/shard_map/place/pallas_call | solution.py:942
